TPU v7x, 128 devices: a whole 4x4x4 slice. The times are simulated.
128 devices in a mesh: ens: 1, slab: 2 (over core), feat: 64 (over z, y, x).
Axes of the slice: x: 4, y: 4, z: 4, core: 2. Of those that a mesh axis runs over, the one named last changes fastest.
Arguments:
- particles: float32 [2048, 65536], P('ens', ('slab', 'feat'))
- prec_diag: float32 [65536], P(('ens', 'slab', 'feat'))
- mean_vec: float32 [65536], P(('ens', 'slab', 'feat'))
- low_rank: bfloat16 [65536, 128], P(('ens', 'slab', 'feat'))
Outputs:
- output: float32 [2048, 65536], P('ens', ('slab', 'feat'))
All inputs are finite; a program needn't handle non-finite values.
Results may differ from a plain program's by a relative error of at most 0.001.
Values are sent between devices in bfloat16 or wider.
A program may use at most 1 GiB of HBM per device.

v0:
```python
import jax
import jax.numpy as jnp
from jax import lax
from jax.sharding import PartitionSpec as P

NUM_STEPS = 3
BAND_SCALE = 4.0
STEP_SCALE = 0.4
FEAT_AXES = ("slab", "feat")
LEAD_AXES = ("ens", "slab", "feat")


def solution(mesh):
    def run_steps(particles, prec_diag, mean_vec, low_rank):
        total_rows, width = particles.shape
        n_part = total_rows // mesh.shape["ens"]
        bandwidth = BAND_SCALE * width
        step_size = STEP_SCALE * width
        rep_coef = 2.0 / bandwidth

        def local_steps(current, prec_loc, mean_loc, fac_loc):
            for step_index in range(NUM_STEPS):
                centered = current - mean_loc[None, :]
                proj_part = jnp.dot(centered.astype(jnp.bfloat16), fac_loc, preferred_element_type=jnp.float32)
                proj_full = lax.psum(proj_part, FEAT_AXES)
                cur_bf = current.astype(jnp.bfloat16)
                gram_part = jnp.einsum("nd,md->nm", cur_bf, cur_bf, preferred_element_type=jnp.float32)
                gram_full = lax.psum(gram_part, FEAT_AXES)
                low_term = jnp.einsum("nr,dr->nd", proj_full.astype(jnp.bfloat16), fac_loc, preferred_element_type=jnp.float32)
                grad_log = -(centered * prec_loc[None, :] + low_term)
                gram_diag = jnp.diagonal(gram_full)
                sq_dist = jnp.maximum(gram_diag[:, None] + gram_diag[None, :] - 2.0 * gram_full, 0.0)
                kernel = jnp.exp(-sq_dist / bandwidth)
                drive_term = grad_log - rep_coef * current
                applied = jnp.dot(kernel.astype(jnp.bfloat16), drive_term.astype(jnp.bfloat16), preferred_element_type=jnp.float32)
                phi_dir = (applied + rep_coef * jnp.sum(kernel, axis=1)[:, None] * current) / n_part
                current = current + step_size * phi_dir
            return current

        sharded = jax.shard_map(
            local_steps,
            mesh=mesh,
            in_specs=(P("ens", FEAT_AXES), P(LEAD_AXES), P(LEAD_AXES), P(LEAD_AXES, None)),
            out_specs=P("ens", FEAT_AXES),
            check_vma=False,
        )
        return sharded(particles, prec_diag, mean_vec, low_rank)

    return run_steps
```

profile of v0, /device:TPU:1, one launch (start us, length us, event | category | flops | bytes accessed | tf_op | source)
XLA Modules:
  0.0 881.1 jit_solution(15989491806024037134)
XLA Ops:
  6.5 0.0 copy-start
  6.5 0.0 all-reduce.7.cloned.1.call-start
  6.5 13.8 %fusion.37 = f32[2048,2048]{1,0:T(8,128)} fusion(f32[2048,512]{1,0:T(8,128)} %param.4), kind=kOutput, calls=%fused_computation.43 | convolution fusion | flops 4296015872 | bytes 20971520 | tf_op jit(solution)/shard_map/nd,md->nm/dot_general | solution.py:27
  20.3 0.0 copy-start.1
  20.3 0.0 all-reduce.7.cloned.1.call-update
  20.3 0.0 all-reduce.9.cloned.1.call-start
  20.4 0.0 copy-done
  20.4 0.6 copy-done.1
  21.0 2.9 fusion.18
  23.9 76.5 %all-reduce.12 = bf16[2048,128]{1,0:T(8,128)(2,1)S(1)} all-reduce(f32[2048,128]{1,0:T(8,128)S(1)} %fusion.18), channel_id=1, replica_groups=mesh['ens'=1,'slab'=2,'feat'=64] {'slab','feat'}, use_global_device_ids=true, to_apply=%region_1.0 | all-reduce | flops 262144 | bytes 1572864 | tf_op jit(solution)/shard_map/psum | solution.py:25
  100.4 139.6 %all-reduce.7.cloned.1.call-done = f32[2048,2048]{1,0:T(8,128)} async-done(((f32[2048,2048]{1,0:T(8,128)}), f32[2048,2048]{1,0:T(8,128)}) %all-reduce.7.cloned.1.call-update) | async-done | bytes 16777232 | tf_op jit(solution)/shard_map/psum | solution.py:28
  240.0 34.1 %gather_fusion = f32[2048]{0:T(1024)S(1)} fusion(f32[2048,2048]{1,0:T(8,128)} %all-reduce.7.cloned.1.call-done, s32[2048]{0:T(1024)S(1)} %bitcast.10), kind=kCustom, calls=%fused_computation | custom fusion | bytes 32768 | tf_op jit(solution)/shard_map/jit(diagonal)/cond/branch_0_fun/gather | solution.py:31
  274.1 0.0 copy-start.2
  274.1 8.5 fusion
  282.6 0.0 copy-done.2
  282.6 16.5 %multiply_add_fusion.2 = f32[2048,512]{1,0:T(8,128)} fusion(f32[2048,512]{1,0:T(8,128)} %param.4, f32[2048,2048]{1,0:T(8,128)} %all-reduce.7.cloned.1.call-done, f32[2048]{0:T(1024)S(1)} %gather_fusion, bf16[512,128]{1,0:T(8,128)(2,1)S(1)} %copy-done, f32[2048]{0:T(1024)S(1)} %broadcast_multiply_fusion.2, f32[512]{0:T(512)S(1)} %copy-done.2, ...), kind=kOutput, calls=%fused_computation.19 | convolution fusion | flops 4604297216 | bytes 25841664 | tf_op jit(solution)/shard_map/dot_general | solution.py:35
  299.1 13.7 %fusion.23 = f32[2048,2048]{1,0:T(8,128)} fusion(f32[2048,512]{1,0:T(8,128)} %multiply_add_fusion.2), kind=kOutput, calls=%fused_computation.29 | convolution fusion | flops 4296015872 | bytes 20971520 | tf_op jit(solution)/shard_map/nd,md->nm/dot_general | solution.py:27
  312.9 0.0 all-reduce.9.cloned.1.call-update
  312.9 0.3 all-reduce.11.cloned.1.call-start
  313.2 2.9 fusion.19
  316.1 72.9 %all-reduce.13 = bf16[2048,128]{1,0:T(8,128)(2,1)S(1)} all-reduce(f32[2048,128]{1,0:T(8,128)S(1)} %fusion.19), channel_id=1, replica_groups=mesh['ens'=1,'slab'=2,'feat'=64] {'slab','feat'}, use_global_device_ids=true, to_apply=%region_4.5 | all-reduce | flops 262144 | bytes 1572864 | tf_op jit(solution)/shard_map/psum | solution.py:25
  389.0 138.3 %all-reduce.9.cloned.1.call-done = f32[2048,2048]{1,0:T(8,128)} async-done(((f32[2048,2048]{1,0:T(8,128)}), f32[2048,2048]{1,0:T(8,128)}) %all-reduce.9.cloned.1.call-update) | async-done | bytes 16777232 | tf_op jit(solution)/shard_map/psum | solution.py:28
  527.4 34.1 %gather_fusion.1 = f32[2048]{0:T(1024)S(1)} fusion(f32[2048,2048]{1,0:T(8,128)} %all-reduce.9.cloned.1.call-done, s32[2048]{0:T(1024)S(1)} %bitcast.11), kind=kCustom, calls=%fused_computation.1 | custom fusion | bytes 32768 | tf_op jit(solution)/shard_map/jit(diagonal)/cond/branch_0_fun/gather | solution.py:31
  561.5 8.5 fusion.2
  570.0 16.7 %multiply_add_fusion.1 = f32[2048,512]{1,0:T(8,128)} fusion(f32[2048,512]{1,0:T(8,128)} %multiply_add_fusion.2, f32[2048,2048]{1,0:T(8,128)} %all-reduce.9.cloned.1.call-done, f32[2048]{0:T(1024)S(1)} %gather_fusion.1, bf16[512,128]{1,0:T(8,128)(2,1)S(1)} %copy-done, f32[2048]{0:T(1024)S(1)} %broadcast_multiply_fusion.1, f32[512]{0:T(512)S(1)} %copy-done.2, ...), kind=kOutput, calls=%fused_computation.17 | convolution fusion | flops 4604297216 | bytes 25841664 | tf_op jit(solution)/shard_map/dot_general | solution.py:35
  586.7 13.7 %fusion.21 = f32[2048,2048]{1,0:T(8,128)} fusion(f32[2048,512]{1,0:T(8,128)} %multiply_add_fusion.1), kind=kOutput, calls=%fused_computation.27 | convolution fusion | flops 4296015872 | bytes 20971520 | tf_op jit(solution)/shard_map/nd,md->nm/dot_general | solution.py:27
  600.5 0.0 all-reduce.11.cloned.1.call-update
  600.5 2.9 fusion.20
  603.4 73.2 %all-reduce.14 = bf16[2048,128]{1,0:T(8,128)(2,1)S(1)} all-reduce(f32[2048,128]{1,0:T(8,128)S(1)} %fusion.20), channel_id=1, replica_groups=mesh['ens'=1,'slab'=2,'feat'=64] {'slab','feat'}, use_global_device_ids=true, to_apply=%region_7.8 | all-reduce | flops 262144 | bytes 1572864 | tf_op jit(solution)/shard_map/psum | solution.py:25
  676.6 138.3 %all-reduce.11.cloned.1.call-done = f32[2048,2048]{1,0:T(8,128)} async-done(((f32[2048,2048]{1,0:T(8,128)}), f32[2048,2048]{1,0:T(8,128)}) %all-reduce.11.cloned.1.call-update) | async-done | bytes 16777232 | tf_op jit(solution)/shard_map/psum | solution.py:28
  814.8 34.1 %gather_fusion.2 = f32[2048]{0:T(1024)S(1)} fusion(f32[2048,2048]{1,0:T(8,128)} %all-reduce.11.cloned.1.call-done, s32[2048]{0:T(1024)S(1)} %bitcast.12), kind=kCustom, calls=%fused_computation.2 | custom fusion | bytes 32768 | tf_op jit(solution)/shard_map/jit(diagonal)/cond/branch_0_fun/gather | solution.py:31
  849.0 8.5 fusion.4
  857.5 16.6 %multiply_add_fusion = f32[2048,512]{1,0:T(8,128)} fusion(f32[2048,512]{1,0:T(8,128)} %multiply_add_fusion.1, f32[2048,2048]{1,0:T(8,128)} %all-reduce.11.cloned.1.call-done, f32[2048]{0:T(1024)S(1)} %gather_fusion.2, bf16[512,128]{1,0:T(8,128)(2,1)S(1)} %copy-done, f32[2048]{0:T(1024)S(1)} %broadcast_multiply_fusion, f32[512]{0:T(512)S(1)} %copy-done.2, ...), kind=kOutput, calls=%fused_computation.15 | convolution fusion | flops 4604297216 | bytes 25841664 | tf_op jit(solution)/shard_map/dot_general | solution.py:35
  (4 shorter events, 0.0 us)
Async XLA Ops:
  6.5 13.9 %copy-start = (bf16[512,128]{1,0:T(8,128)(2,1)S(1)}, bf16[512,128]{1,0:T(8,128)(2,1)}, u32[]{:S(2)}) copy-start(bf16[512,128]{1,0:T(8,128)(2,1)} %param.7) | copy-start | bytes 393220
  6.5 233.4 %all-reduce.7.cloned.1.call-start = ((), (), s32[]{:S(2)}) async-start(), calls=%async_computation | async-start | bytes 33554432 | tf_op jit(solution)/shard_map/psum | solution.py:28
  20.3 0.7 copy-start.1
  20.3 507.0 %all-reduce.9.cloned.1.call-start = ((), (), s32[]{:S(2)}) async-start(), calls=%async_computation.1 | async-start | bytes 33554432 | tf_op jit(solution)/shard_map/psum | solution.py:28
  274.1 8.5 copy-start.2
  312.9 501.9 %all-reduce.11.cloned.1.call-start = ((), (), s32[]{:S(2)}) async-start(), calls=%async_computation.2 | async-start | bytes 33554432 | tf_op jit(solution)/shard_map/psum | solution.py:28
Sparse Core Ops, SparseCore 0:
  20.5 219.4 all-reduce.6
  313.0 214.2 all-reduce.8
  600.6 214.1 all-reduce.10
where the time goes:
time: 889 us; the launch traced here: 881 us
  waiting for transfers between devices  416 us (47%)
  blocking collectives  223 us (25%)
  local copies, waits for them, and re-layouts  103 us (12%)
  matrix products  99.8 us (11%)
  other arithmetic  25.5 us (3%)
  between operations  13.7 us (2%)
    psum x3, waiting for transfers between devices, local_steps(): gram_full = lax.psum(gram_part, FEAT_AXES)  416 us
    psum x3, blocking collectives, local_steps(): proj_full = lax.psum(proj_part, FEAT_AXES)  223 us
    gather x3, local copies, waits for them, and re-layouts, local_steps(): gram_diag = jnp.diagonal(gram_full)  102 us
    dot_general x3, matrix products, local_steps(): jnp.dot(kernel.astype(jnp.bfloat16), drive_term.astype(jnp.bfloat16), pre...  49.9 us
    dot_general x3, matrix products, local_steps(): jnp.einsum('nd,md->nm', cur_bf, cur_bf, preferred_element_type=jnp.float32)  41.3 us
    reduce_sum x3, other arithmetic, local_steps(): jnp.sum(kernel, axis=1)[:, None]  25.5 us
  transfers between devices with their start and end apart: 3, of which 3 were waited for; matrix products, arithmetic and copies ran while one was open for 1% of the time, Pallas kernels for 0%

commit v1 on v0

v1 whole, which is shorter than its diff:
```python
import functools

import jax
import jax.numpy as jnp
from jax import lax
from jax.experimental import pallas as pl
from jax.experimental.pallas import tpu as pltpu
from jax.sharding import PartitionSpec as P

NUM_STEPS = 3
BAND_SCALE = 4.0
STEP_SCALE = 0.4
FEAT_AXES = ("slab", "feat")
LEAD_AXES = ("ens", "slab", "feat")

ROWS = 2048
TILE = 128
BLK = 512
COLORS = 6
SROWS = COLORS * BLK
UNITS = (None, ((0, 1), (0, 2), (0, 3)), ((1, 2), (1, 3), (2, 3)))
OFFS = (((0, 1), (0, 2), (0, 3)), ((1, 2), (1, 3), (2, 3)))
PM_ROW = 4 * BLK
OWN = 32
MESH = pl.DeviceIdType.MESH
NT = (((1,), (1,)), ((), ()))
F32, BF16 = jnp.float32, jnp.bfloat16


def div(a, b):
    return lax.div(a, jnp.int32(b))


def rem(a, b):
    return lax.rem(a, jnp.int32(b))


def _kernel(
    bandwidth, step_size, n_part,
    theta_ref, lam_ref, mu_ref, fac_ref, out_ref,
    bfull, pml, pmr, nrow, ncol, srow, pack, r0, r1, r2, r3, kg, kfull, adrv, svec, srecv, stot, spart,
    pre_send, pre_recv, rs_send, rs_recv, x_send, x_recv, dd_send, dd_recv, s_send, s_recv, sp_send, sp_recv,
):
    width = theta_ref.shape[1]
    rep_coef = 2.0 / bandwidth
    core = lax.axis_index("slab")
    feat = lax.axis_index("feat")
    coords = (rem(feat, 4), rem(div(feat, 4), 4), div(feat, 16))
    strides = (1, 4, 16)

    def chip(dim, coord):
        return {"feat": feat + (coord - coords[dim]) * strides[dim]}

    turned = [[coords[dim]] + [rem(coords[dim] + j, 4) for j in range(1, 4)] for dim in range(3)]

    def around(dim, j):
        return turned[dim][j]

    ring = [[chip(dim, turned[dim][j]) for j in range(4)] for dim in range(3)]
    low_bit = [rem(c, 2) for c in coords]
    pair_bit = [[rem(div(t + 1, 2), 2) for t in turned[dim]] for dim in range(3)]
    high_bit = [[div(t, 2) for t in turned[dim]] for dim in range(3)]

    mate = {"slab": 1 - core}

    def al(x, m=16):
        return pl.multiple_of(x, m)

    halves = []
    for k in range(COLORS):
        steps = []
        start, length, cur = 0, BLK, coords[k % 3]
        for s in range(2):
            if (k // 3 + s) % 2 == 0:
                other, bit = cur + 1 - 2 * low_bit[k % 3], pair_bit[k % 3][0]
            else:
                other, bit = 3 - cur, high_bit[k % 3][0]
            length = length // 2
            keep, give = start + bit * length, start + (1 - bit) * length
            start = keep
            steps.append((chip(k % 3, other), length, keep, give))
        halves.append(steps)

    def dims(k):
        return k % 3, (k + 1) % 3, (k + 2) % 3

    def base(st, k):
        return st * SROWS + k * BLK

    quarters = [[base(st, k) + halves[k][1][2] for k in range(COLORS)] for st in range(3)]
    owns = [[quarters[st][k] + OWN * coords[dims(k)[1]] for k in range(COLORS)] for st in range(3)]
    pieces = [[OWN * around(dims(k)[1], j) for j in range(4)] for k in range(COLORS)]

    places = []
    for k in range(COLORS):
        one, two = (pair_bit, high_bit) if k < 3 else (high_bit, pair_bit)
        places.append([TILE * (2 * one[k % 3][j] + two[k % 3][j]) for j in range(4)])

    def quarter(st, k):
        return quarters[st][k]

    def own(st, k):
        return owns[st][k]

    barrier = pltpu.get_barrier_semaphore()
    pl.semaphore_signal(barrier, inc=1, device_id=mate, device_id_type=MESH)
    for dim in range(3):
        for j in range(1, 4):
            pl.semaphore_signal(barrier, inc=1, device_id=ring[dim][j], device_id_type=MESH)
    pl.semaphore_wait(barrier, 10)

    row_i = lax.broadcasted_iota(jnp.int32, (TILE, TILE), 0)
    col_i = lax.broadcasted_iota(jnp.int32, (TILE, TILE), 1)
    eye, upper, lower = row_i == col_i, row_i < col_i, row_i > col_i
    sub_o = lax.broadcasted_iota(jnp.int32, (OWN, TILE), 0)
    lane_o = lax.broadcasted_iota(jnp.int32, (OWN, TILE), 1)

    def remote(src, dst, ssem, rsem, where):
        return pltpu.make_async_remote_copy(src_ref=src, dst_ref=dst, send_sem=ssem, recv_sem=rsem, device_id=where, device_id_type=MESH)

    def pre_copy(ch, what):
        if what == 0:
            rows = pl.ds(ch * BLK, BLK)
            src, dst = bfull.at[rows, 0:width], bfull.at[rows, width:2 * width]
        else:
            src, dst = pml.at[pl.ds(al(ch * BLK + (1 - core) * 256), 256)], pmr.at[pl.ds(ch * 256, 256)]
        return remote(src, dst, pre_send.at[what, ch], pre_recv.at[what, ch], mate)

    def prepare(ch, th):
        rows = pl.ds(ch * BLK, BLK)
        bfull[rows, 0:width] = th.astype(BF16)
        pml[rows, :] = jnp.dot((th - mu_ref[...]).astype(BF16), fac_ref[...], preferred_element_type=F32)

    for ch in range(4):
        rows = pl.ds(ch * BLK, BLK)
        th = theta_ref[rows, :]
        out_ref[rows, :] = th
        prepare(ch, th)
        for what in range(2):
            pre_copy(ch, what).start()

    def one_step(step_index, carry):
        sends = []

        def begin(cps):
            for cp in cps:
                cp.start()
            sends.extend(cps)

        def rs_copy(st, s, k):
            peer, length, keep, give = halves[k][s]
            src = pack.at[pl.ds(al(base(st, k) + give), length)]
            return remote(src, (r0, r1)[s].at[st, k], rs_send.at[st, s, k], rs_recv.at[st, s, k], peer)

        def x_copies(st, e, k):
            d1, d2, d3 = dims(k)
            dim = (d2, d3, d2, d1)[e]
            cps = []
            for j in range(1, 4):
                if e == 0:
                    src = pack.at[pl.ds(al(quarter(st, k) + pieces[k][j]), OWN)]
                    dst = r2.at[st, k, j - 1]
                elif e == 1:
                    src = dst = r3.at[st, k, coords[dim]]
                else:
                    rng = pl.ds(al(own(st, k)), OWN) if e == 2 else pl.ds(al(quarter(st, k)), TILE)
                    src = dst = kg.at[core, rng]
                cps.append(remote(src, dst, x_send.at[st, e, k, j - 1], x_recv.at[st, e, k, j - 1], ring[dim][j]))
            return cps

        def dd_copy(st, k, j):
            if j == 0:
                begin_row = quarter(st, k)
            else:
                begin_row = base(st, k) + places[k][4 - j]
            rng = pl.ds(al(begin_row), TILE)
            return remote(kg.at[core, rng], kg.at[core, rng], dd_send.at[st, k, j], dd_recv.at[st, k, j], mate)

        def s_copies(st, ph, d):
            dim = ((d + 1) % 3, d)[ph]
            return [
                remote(svec.at[st, ph, d], srecv.at[st, ph, d, j - 1], s_send.at[st, ph, d, j - 1], s_recv.at[st, ph, d, j - 1], ring[dim][j])
                for j in range(1, 4)
            ]

        def sp_copy(st):
            return remote(stot.at[st], spart.at[st], sp_send.at[st], sp_recv.at[st], mate)

        def diag_tiles(sup):
            bb = bfull[pl.ds(sup * BLK, BLK), :]
            g = lax.dot_general(bb, bb, NT, preferred_element_type=F32)

            def tile(i, j):
                return g[i * TILE:(i + 1) * TILE, j * TILE:(j + 1) * TILE]

            rows_n, cols_n = [], []
            for i in range(4):
                d = jnp.where(eye, tile(i, i), 0.0)
                rows_n.append(jnp.broadcast_to(jnp.sum(d, axis=1, keepdims=True), (TILE, TILE)))
                cols_n.append(jnp.sum(d, axis=0, keepdims=True))
                nrow[pl.ds((4 * sup + i) * TILE, TILE), :] = rows_n[i]
                ncol[pl.ds(4 * sup + i, 1), :] = cols_n[i]

            def dist(i, j):
                return rows_n[i] + cols_n[j] - 2.0 * tile(i, j)

            for t in range(3):
                pack[pl.ds(base(0, sup) + t * TILE, TILE), :] = jnp.where(core == 0, dist(*OFFS[0][t]), dist(*OFFS[1][t]))
            one = jnp.where(core == 0, dist(0, 0), dist(2, 2))
            two = jnp.where(core == 0, dist(1, 1), dist(3, 3))
            pack[pl.ds(base(0, sup) + 3 * TILE, TILE), :] = jnp.where(upper, one, two)

        def unit_tiles(st, u):
            sup, m = UNITS[st][u]
            lhs = bfull[pl.ds(sup * BLK, BLK), :]
            rhs = bfull[pl.ds(al((2 * m + core) * 256), 256), :]
            g = lax.dot_general(lhs, rhs, NT, preferred_element_type=F32)
            for b in range(2):
                nc = ncol[pl.ds(4 * m + 2 * core + b, 1), :]
                pack[pl.ds(base(st, 2 * u + b), BLK), :] = nrow[pl.ds(sup * BLK, BLK), :] + nc - 2.0 * g[:, b * TILE:(b + 1) * TILE]

        def row_sums(st, k, kern):
            place = own(0, k) - base(0, k)
            slot, r = div(place, TILE), rem(place, TILE)

            def by_rows(vals):
                rs = jnp.sum(vals, axis=1, keepdims=True)
                return jnp.sum(jnp.where(lane_o == sub_o + r, rs, 0.0), axis=0, keepdims=True)

            def by_cols(vals):
                return jnp.sum(vals, axis=0, keepdims=True)

            if st > 0:
                sup, m = UNITS[st][k // 2]
                return [(4 * sup + slot, by_rows(kern)), (4 * m + 2 * core + k % 2, by_cols(kern))]
            both = div(slot, 3)
            i0 = (1 - both) * core * (1 + div(slot, 2)) + both * 2 * core
            j0 = (1 - both) * ((1 - core) * (slot + 1) + core * (2 + div(slot + 1, 2))) + both * 2 * core
            up = jnp.where(lane_o + 1000 * (1 - both) > sub_o + r, kern, 0.0)
            lo = jnp.where(lane_o + 1000 * (1 - both) < sub_o + r, kern, 0.0)
            nxt = 4 * k + 2 * core + 1
            return [(4 * k + i0, by_rows(up)), (4 * k + j0, by_cols(up)), (nxt, by_rows(lo)), (nxt, by_cols(lo))]

        def advance(st, s):
            parts = [[], [], []]
            for k in range(COLORS):
                mine = pl.ds(al(own(st, k)), OWN)
                if s < 2:
                    peer, length, keep, give = halves[k][s]
                    rs_copy(st, s, k).wait_recv()
                    rng = pl.ds(al(base(st, k) + keep), length)
                    pack[rng, :] += (r0, r1)[s][st, k]
                    begin([rs_copy(st, 1, k)] if s == 0 else x_copies(st, 0, k))
                elif s == 2:
                    for cp in x_copies(st, 0, k):
                        cp.wait_recv()
                    r3[st, k, coords[dims(k)[2]]] = pack[mine, :] + r2[st, k, 0] + r2[st, k, 1] + r2[st, k, 2]
                    begin(x_copies(st, 1, k))
                elif s == 3:
                    for cp in x_copies(st, 1, k):
                        cp.wait_recv()
                    full = (r3[st, k, 0] + r3[st, k, 1]) + (r3[st, k, 2] + r3[st, k, 3])
                    if st == 0 and k >= 4:
                        kern = full
                    else:
                        kern = jnp.exp(-jnp.maximum(full, 0.0) / bandwidth)
                        parts[k % 3] += row_sums(st, k, kern)
                    kg[core, mine, :] = kern.astype(BF16)
                    begin(x_copies(st, 2, k))
                elif s == 4:
                    for cp in x_copies(st, 2, k):
                        cp.wait_recv()
                    begin(x_copies(st, 3, k))
                    begin([dd_copy(st, k, 0)])
                else:
                    for j, cp in enumerate(x_copies(st, 3, k)):
                        cp.wait_recv()
                        begin([dd_copy(st, k, j + 1)])
            if s == 3:
                for d in range(3):
                    svec[st, 0, d] = jnp.zeros((16, TILE), F32)
                    for block, line in parts[d]:
                        svec[st, 0, d, pl.ds(block, 1), :] += line
                    begin(s_copies(st, 0, d))
            if s == 4:
                for d in range(3):
                    for cp in s_copies(st, 0, d):
                        cp.wait_recv()
                    svec[st, 1, d] = svec[st, 0, d] + srecv[st, 0, d, 0] + srecv[st, 0, d, 1] + srecv[st, 0, d, 2]
                    begin(s_copies(st, 1, d))
            if s == 5:
                tot = jnp.zeros((16, TILE), F32)
                for d in range(3):
                    for cp in s_copies(st, 1, d):
                        cp.wait_recv()
                    tot = tot + ((svec[st, 1, d] + srecv[st, 1, d, 0]) + (srecv[st, 1, d, 1] + srecv[st, 1, d, 2]))
                stot[st] = tot
                begin([sp_copy(st)])

        def unpack(st):
            for k in range(COLORS):
                for j in range(4):
                    dd_copy(st, k, j).wait_recv()
            for c in range(2):
                if st > 0:
                    for k in range(COLORS):
                        sup, m = UNITS[st][k // 2]
                        src = kg[c, pl.ds(base(st, k), BLK), :]
                        jcol = pl.ds((4 * m + 2 * c + k % 2) * TILE, TILE)
                        kfull[pl.ds(sup * BLK, BLK), jcol] = src
                        kfull[jcol, pl.ds(sup * BLK, BLK)] = src.T
                    continue
                for sup in range(4):
                    for t, (i, j) in enumerate(OFFS[c]):
                        src = kg[c, pl.ds(base(0, sup) + t * TILE, TILE), :]
                        ri, rj = pl.ds((4 * sup + i) * TILE, TILE), pl.ds((4 * sup + j) * TILE, TILE)
                        kfull[ri, rj] = src
                        kfull[rj, ri] = src.T
                    src = kg[c, pl.ds(base(0, sup) + 3 * TILE, TILE), :]
                    srt = src.T
                    one = jnp.ones((TILE, TILE), BF16)
                    ra, rb = pl.ds((4 * sup + 2 * c) * TILE, TILE), pl.ds((4 * sup + 2 * c + 1) * TILE, TILE)
                    kfull[ra, ra] = jnp.where(upper, src, jnp.where(lower, srt, one))
                    kfull[rb, rb] = jnp.where(lower, src, jnp.where(upper, srt, one))

        def drive():
            for q in range(8):
                rows = pl.ds(q * 256, 256)
                pm = kg[q % 2, pl.ds(PM_ROW + (q // 2) * 256, 256), :]
                low = lax.dot_general(pm, fac_ref[...], NT, preferred_element_type=F32)
                th = out_ref[rows, :]
                grad = -((th - mu_ref[...]) * lam_ref[...] + low)
                adrv[rows, :] = (grad - rep_coef * th).astype(BF16)

        def sum_rows(blocks):
            tot = stot[0] + spart[0] + stot[1] + spart[1] + 1.0
            if len(blocks) > 4:
                tot = tot + (stot[2] + spart[2])
            for blk in blocks:
                line = jnp.sum(jnp.where(eye, jnp.broadcast_to(tot[blk:blk + 1, :], (TILE, TILE)), 0.0), axis=1, keepdims=True)
                srow[pl.ds(blk * TILE, TILE), :] = jnp.broadcast_to(rep_coef * line, (TILE, TILE))

        def update(ch):
            rows = pl.ds(ch * BLK, BLK)
            acc = jnp.dot(kfull[rows, :], adrv[...], preferred_element_type=F32)
            new = []
            for t in range(width // TILE):
                cols = slice(t * TILE, (t + 1) * TILE)
                th = out_ref[rows, cols]
                phi = (acc[:, cols] + srow[rows, :] * th) / n_part
                new.append(th + step_size * phi)
            th = jnp.concatenate(new, axis=1)
            out_ref[rows, :] = th
            prepare(ch, th)

            @pl.when(step_index < NUM_STEPS - 1)
            def _():
                for what in range(2):
                    pre_copy(ch, what).start()

        for ch in range(4):
            pre_copy(ch, 1).wait_recv()
            mine = pl.ds(al(ch * BLK + core * 256), 256)
            pack[pl.ds(PM_ROW + ch * 256, 256), :] = pml[mine, :] + pmr[pl.ds(ch * 256, 256), :]
            if ch % 2 == 1:
                begin([rs_copy(0, 0, 4 + ch // 2)])
        for sup in range(4):
            pre_copy(sup, 0).wait_recv()
            diag_tiles(sup)
            begin([rs_copy(0, 0, sup)])
        for st in (1, 2):
            for u in range(3):
                unit_tiles(st, u)
                begin([rs_copy(st, 0, 2 * u), rs_copy(st, 0, 2 * u + 1)])
        for s in range(5):
            for st in range(3):
                advance(st, s)
        advance(0, 5)
        advance(1, 5)
        unpack(0)
        drive()
        advance(2, 5)
        for ch in range(4):
            for what in range(2):
                pre_copy(ch, what).wait_send()
        sp_copy(0).wait_recv()
        sp_copy(1).wait_recv()
        sum_rows(range(4))
        unpack(1)
        update(0)
        sp_copy(2).wait_recv()
        sum_rows(range(4, 16))
        unpack(2)
        for ch in range(1, 4):
            update(ch)
        for cp in sends:
            cp.wait_send()
        return carry

    lax.fori_loop(0, NUM_STEPS, one_step, 0)


def solution(mesh):
    def run_steps(particles, prec_diag, mean_vec, low_rank):
        total_rows, width = particles.shape
        n_part = total_rows // mesh.shape["ens"]
        bandwidth = BAND_SCALE * width
        step_size = STEP_SCALE * width
        loc = width // (mesh.shape["slab"] * mesh.shape["feat"])
        rank = low_rank.shape[1]
        vm, dma = pltpu.VMEM, pltpu.SemaphoreType.DMA

        def local_steps(current, prec_loc, mean_loc, fac_loc):
            spec = pl.BlockSpec(memory_space=pltpu.VMEM)
            call = pl.pallas_call(
                functools.partial(_kernel, bandwidth, step_size, n_part),
                out_shape=jax.ShapeDtypeStruct((n_part, loc), F32),
                in_specs=[spec] * 4,
                out_specs=spec,
                scratch_shapes=[
                    vm((ROWS, 2 * loc), BF16), vm((ROWS, rank), F32), vm((ROWS // 2, rank), F32),
                    vm((ROWS, TILE), F32), vm((16, TILE), F32), vm((ROWS, TILE), F32),
                    vm((3 * SROWS, TILE), F32),
                    vm((3, COLORS, BLK // 2, TILE), F32), vm((3, COLORS, BLK // 4, TILE), F32),
                    vm((3, COLORS, 3, OWN, TILE), F32), vm((3, COLORS, 4, OWN, TILE), F32),
                    vm((2, 3 * SROWS, TILE), BF16), vm((ROWS, ROWS), BF16), vm((ROWS, loc), BF16),
                    vm((3, 2, 3, 16, TILE), F32), vm((3, 2, 3, 3, 16, TILE), F32), vm((3, 16, TILE), F32), vm((3, 16, TILE), F32),
                    dma((2, 4)), dma((2, 4)), dma((3, 2, COLORS)), dma((3, 2, COLORS)), dma((3, 4, COLORS, 3)), dma((3, 4, COLORS, 3)),
                    dma((3, COLORS, 4)), dma((3, COLORS, 4)), dma((3, 2, 3, 3)), dma((3, 2, 3, 3)), dma((3,)), dma((3,)),
                ],
                compiler_params=pltpu.CompilerParams(collective_id=0, has_side_effects=True, vmem_limit_bytes=62 * 1024 * 1024),
                name="svgd",
            )
            return call(current, prec_loc.reshape(1, loc), mean_loc.reshape(1, loc), fac_loc)

        sharded = jax.shard_map(
            local_steps,
            mesh=mesh,
            in_specs=(P("ens", FEAT_AXES), P(LEAD_AXES), P(LEAD_AXES), P(LEAD_AXES, None)),
            out_specs=P("ens", FEAT_AXES),
            check_vma=False,
        )
        return sharded(particles, prec_diag, mean_vec, low_rank)

    return run_steps
```

time: 889 us -> 176 us (0.20)
  waiting for transfers between devices: 416 us -> 0 us
  blocking collectives: 223 us -> 0 us
  Pallas kernels: 0 us -> 171 us
  matrix products: 99.8 us -> 0 us
  local copies, waits for them, and re-layouts: 103 us -> 4.64 us
  other arithmetic: 25.5 us -> 0 us
  between operations: 13.7 us -> 0.01 us
    psum x3 -> x0, waiting for transfers between devices: 416 us -> none  [local_steps(): gram_full = lax.psum(gram_part, FEAT_AXES)]
    psum x3 -> x0, blocking collectives: 223 us -> none  [local_steps(): proj_full = lax.psum(proj_part, FEAT_AXES)]
    pallas_call x0 -> x1, Pallas kernels: none -> 171 us  [local_steps(): call(current, prec_loc.reshape(1, loc), mean_loc.reshape(1, loc), fac_loc)]
    gather x3 -> x0, local copies, waits for them, and re-layouts: 102 us -> none  [local_steps(): gram_diag = jnp.diagonal(gram_full)]
    dot_general x9 -> x0, matrix products: 99.8 us -> none  [the longest x3 49.9 us: local_steps(): jnp.dot(kernel.astype(jnp.bfloat16), drive_term.astype(jnp.bfloat16), pre...]
    reduce_sum x3 -> x0, other arithmetic: 25.5 us -> none  [local_steps(): jnp.sum(kernel, axis=1)[:, None]]
  transfers between devices with their start and end apart: 3 -> 0, of which waited for: 3 -> 0; matrix products, arithmetic and copies ran while one was open for 1% -> 0% of each run, Pallas kernels for 0% -> 0%
where the time goes in v1:
time: 176 us
  Pallas kernels  171 us (97%)
  local copies, waits for them, and re-layouts  4.64 us (3%)
    pallas_call x1, Pallas kernels, local_steps(): call(current, prec_loc.reshape(1, loc), mean_loc.reshape(1, loc), fac_loc)  171 us
    unnamed x1, local copies, waits for them, and re-layouts  4.64 us

profile of v1, /device:TPU:1, one launch (start us, length us, event | category | flops | bytes accessed | tf_op | source)
XLA Modules:
  0.0 175.6 jit_solution(17633626147970071965)
XLA Ops:
  0.0 170.9 %svgd.1 = f32[2048,512]{1,0:T(8,128)} custom-call(f32[2048,512]{1,0:T(8,128)} %theta_ref.1, f32[1,512]{1,0:T(1,128)} %bitcast.2, f32[1,512]{1,0:T(1,128)} %bitcast.3, bf16[512,128]{1,0:T(8,128)(2,1)} %fac_ref.1), custom_call_target="tpu_custom_call" | custom-call | tf_op jit(solution)/shard_map/svgd/pallas_call | solution.py:434
  171.0 4.6 %copy.6 = f32[2048,512]{1,0:T(8,128)} copy(f32[2048,512]{1,0:T(8,128)} %svgd.1) | data formatting | bytes 8388608

commit v2 on v1

v2 whole, which is shorter than its diff:
```python
import functools

import jax
import jax.numpy as jnp
from jax import lax
from jax.experimental import pallas as pl
from jax.experimental.pallas import tpu as pltpu
from jax.sharding import PartitionSpec as P

NUM_STEPS = 3
BAND_SCALE = 4.0
STEP_SCALE = 0.4
FEAT_AXES = ("slab", "feat")
LEAD_AXES = ("ens", "slab", "feat")

ROWS = 2048
TILE = 128
BLK = 512
COLORS = 6
SROWS = COLORS * BLK
UNITS = (None, ((0, 1), (0, 2), (0, 3)), ((1, 2), (1, 3), (2, 3)))
OFFS = (((0, 1), (0, 2), (0, 3)), ((1, 2), (1, 3), (2, 3)))
PM_ROW = 4 * BLK
SENT = 1536 + 768 + 576 + 576 + 288 + 1152 + 1536 + 288 + 16
OWN = 32
MESH = pl.DeviceIdType.MESH
NT = (((1,), (1,)), ((), ()))
F32, BF16 = jnp.float32, jnp.bfloat16


def div(a, b):
    return lax.div(a, jnp.int32(b))


def rem(a, b):
    return lax.rem(a, jnp.int32(b))


def _kernel(
    bandwidth, step_size, n_part,
    theta_ref, lam_ref, mu_ref, fac_ref, out_ref,
    bfull, pml, pmr, nrow, ncol, srow, pack, r0, r1, r2, r3, kg, kfull, adrv, svec, srecv, stot, spart,
    in_sem, pre_send, pre_recv, sent, rs_recv, x_recv, far_recv, dd_recv, s_recv, sp_recv,
):
    width = out_ref.shape[1]
    rep_coef = 2.0 / bandwidth
    core = lax.axis_index("slab")
    feat = lax.axis_index("feat")
    coords = (rem(feat, 4), rem(div(feat, 4), 4), div(feat, 16))
    strides = (1, 4, 16)

    def chip(dim, coord):
        return {"feat": feat + (coord - coords[dim]) * strides[dim]}

    turned = [[coords[dim]] + [rem(coords[dim] + j, 4) for j in range(1, 4)] for dim in range(3)]

    def around(dim, j):
        return turned[dim][j]

    ring = [[chip(dim, turned[dim][j]) for j in range(4)] for dim in range(3)]
    low_bit = [rem(c, 2) for c in coords]
    pair_bit = [[rem(div(t + 1, 2), 2) for t in turned[dim]] for dim in range(3)]
    high_bit = [[div(t, 2) for t in turned[dim]] for dim in range(3)]

    mate = {"slab": 1 - core}

    def al(x, m=16):
        return pl.multiple_of(x, m)

    halves = []
    for k in range(COLORS):
        steps = []
        start, length, cur = 0, BLK, coords[k % 3]
        for s in range(2):
            if (k // 3 + s) % 2 == 0:
                other, bit = cur + 1 - 2 * low_bit[k % 3], pair_bit[k % 3][0]
            else:
                other, bit = 3 - cur, high_bit[k % 3][0]
            length = length // 2
            keep, give = start + bit * length, start + (1 - bit) * length
            start = keep
            steps.append((chip(k % 3, other), length, keep, give))
        halves.append(steps)

    def dims(k):
        return k % 3, (k + 1) % 3, (k + 2) % 3

    def base(st, k):
        return st * SROWS + k * BLK

    quarters = [[base(st, k) + halves[k][1][2] for k in range(COLORS)] for st in range(3)]
    owns = [[quarters[st][k] + OWN * coords[dims(k)[1]] for k in range(COLORS)] for st in range(3)]
    pieces = [[OWN * around(dims(k)[1], j) for j in range(4)] for k in range(COLORS)]

    places = []
    for k in range(COLORS):
        one, two = (pair_bit, high_bit) if k < 3 else (high_bit, pair_bit)
        places.append([TILE * (2 * one[k % 3][j] + two[k % 3][j]) for j in range(4)])

    def quarter(st, k):
        return quarters[st][k]

    def own(st, k):
        return owns[st][k]

    barrier = pltpu.get_barrier_semaphore()
    pl.semaphore_signal(barrier, inc=1, device_id=mate, device_id_type=MESH)
    for dim in range(3):
        for j in range(1, 4):
            pl.semaphore_signal(barrier, inc=1, device_id=ring[dim][j], device_id_type=MESH)
    loads = [pltpu.make_async_copy(theta_ref.at[pl.ds(ch * BLK, BLK)], out_ref.at[pl.ds(ch * BLK, BLK)], in_sem.at[ch]) for ch in range(4)]
    for cp in loads:
        cp.start()

    row_i = lax.broadcasted_iota(jnp.int32, (TILE, TILE), 0)
    col_i = lax.broadcasted_iota(jnp.int32, (TILE, TILE), 1)
    eye, upper, lower = row_i == col_i, row_i < col_i, row_i > col_i
    sub_o = lax.broadcasted_iota(jnp.int32, (OWN, TILE), 0)
    lane_o = lax.broadcasted_iota(jnp.int32, (OWN, TILE), 1)

    def remote(src, dst, ssem, rsem, where):
        return pltpu.make_async_remote_copy(src_ref=src, dst_ref=dst, send_sem=ssem, recv_sem=rsem, device_id=where, device_id_type=MESH)

    def pre_copy(ch, what):
        if what == 0:
            rows = pl.ds(ch * BLK, BLK)
            src, dst = bfull.at[rows, 0:width], bfull.at[rows, width:2 * width]
        else:
            src, dst = pml.at[pl.ds(al(ch * BLK + (1 - core) * 256), 256)], pmr.at[pl.ds(ch * 256, 256)]
        return remote(src, dst, pre_send, pre_recv.at[what, ch], mate)

    def prepare(start, length, th):
        rows = pl.ds(start, length)
        bfull[rows, 0:width] = th.astype(BF16)
        pml[rows, :] = jnp.dot((th - mu_ref[...]).astype(BF16), fac_ref[...], preferred_element_type=F32)

    def begin(cps):
        for cp in cps:
            cp.start()

    def arrive(ref, sem):
        remote(ref, ref, sent.at[0], sem, mate).wait_recv()

    def x_arrive(st, e, k):
        arrive((r2.at[st, k], r3.at[st, k, 0:3], kg.at[core, 0:3 * OWN])[e], x_recv.at[st, e, k])

    def rs_copy(st, s, k):
        peer, length, keep, give = halves[k][s]
        src = pack.at[pl.ds(al(base(st, k) + give), length)]
        return remote(src, (r0, r1)[s].at[st, k], sent.at[st], rs_recv.at[st, s, k], peer)

    def x_copies(st, e, k):
        d1, d2, d3 = dims(k)
        dim = (d2, d3, d2, d1)[e]
        cps = []
        for j in range(1, 4):
            if e == 0:
                src = pack.at[pl.ds(al(quarter(st, k) + pieces[k][j]), OWN)]
                dst = r2.at[st, k, j - 1]
            elif e == 1:
                src = dst = r3.at[st, k, coords[dim]]
            else:
                rng = pl.ds(al(own(st, k)), OWN) if e == 2 else pl.ds(al(quarter(st, k)), TILE)
                src = dst = kg.at[core, rng]
            arrived = far_recv.at[st, k, j - 1] if e == 3 else x_recv.at[st, e, k]
            cps.append(remote(src, dst, sent.at[st], arrived, ring[dim][j]))
        return cps

    def dd_copy(st, k, j):
        if j == 0:
            begin_row = quarter(st, k)
        else:
            begin_row = base(st, k) + places[k][4 - j]
        rng = pl.ds(al(begin_row), TILE)
        return remote(kg.at[core, rng], kg.at[core, rng], sent.at[st], dd_recv.at[st, k], mate)

    def s_copies(st, ph, d):
        dim = ((d + 1) % 3, d)[ph]
        return [
            remote(svec.at[st, ph, d], srecv.at[st, ph, d, j - 1], sent.at[st], s_recv.at[st, ph, d], ring[dim][j])
            for j in range(1, 4)
        ]

    def sp_copy(st):
        return remote(stot.at[st], spart.at[st], sent.at[st], sp_recv.at[st], mate)

    def diag_tiles(sup):
        bb = bfull[pl.ds(sup * BLK, BLK), :]
        g = lax.dot_general(bb, bb, NT, preferred_element_type=F32)

        def tile(i, j):
            return g[i * TILE:(i + 1) * TILE, j * TILE:(j + 1) * TILE]

        rows_n, cols_n = [], []
        for i in range(4):
            d = jnp.where(eye, tile(i, i), 0.0)
            rows_n.append(jnp.broadcast_to(jnp.sum(d, axis=1, keepdims=True), (TILE, TILE)))
            cols_n.append(jnp.sum(d, axis=0, keepdims=True))
            nrow[pl.ds((4 * sup + i) * TILE, TILE), :] = rows_n[i]
            ncol[pl.ds(4 * sup + i, 1), :] = cols_n[i]

        def dist(i, j):
            return rows_n[i] + cols_n[j] - 2.0 * tile(i, j)

        for t in range(3):
            pack[pl.ds(base(0, sup) + t * TILE, TILE), :] = jnp.where(core == 0, dist(*OFFS[0][t]), dist(*OFFS[1][t]))
        one = jnp.where(core == 0, dist(0, 0), dist(2, 2))
        two = jnp.where(core == 0, dist(1, 1), dist(3, 3))
        pack[pl.ds(base(0, sup) + 3 * TILE, TILE), :] = jnp.where(upper, one, two)

    def pm_tiles():
        for ch in range(4):
            pre_copy(ch, 1).wait_recv()
            mine = pl.ds(al(ch * BLK + core * 256), 256)
            pack[pl.ds(PM_ROW + ch * 256, 256), :] = pml[mine, :] + pmr[pl.ds(ch * 256, 256), :]
        begin([rs_copy(0, 0, 4), rs_copy(0, 0, 5)])

    def open_step():
        for sup in range(4):
            pre_copy(sup, 0).wait_recv()
            diag_tiles(sup)
            begin([rs_copy(0, 0, sup)])
            if sup == 2:
                pm_tiles()

    for ch in range(4):
        loads[ch].wait()
        prepare(ch * BLK, BLK, out_ref[pl.ds(ch * BLK, BLK), :])
    pl.semaphore_wait(barrier, 10)
    for ch in range(4):
        begin([pre_copy(ch, 1), pre_copy(ch, 0)])
    open_step()

    def one_step(step_index, carry):
        def unit_tiles(st, units):
            sup = UNITS[st][units[0]][0]
            blocks = [4 * UNITS[st][u][1] + 2 * core for u in units]
            lhs = jnp.concatenate([bfull[pl.ds(al(blk * TILE), 256), :] for blk in blocks], axis=0)
            g = lax.dot_general(lhs, bfull[pl.ds(sup * BLK, BLK), :], NT, preferred_element_type=F32)
            for n, u in enumerate(units):
                for b in range(2):
                    nr = nrow[pl.ds(al((blocks[n] + b) * TILE), TILE), :]
                    for a in range(4):
                        tile = g[n * 256 + b * TILE:n * 256 + (b + 1) * TILE, a * TILE:(a + 1) * TILE]
                        pack[pl.ds(base(st, 2 * u + b) + a * TILE, TILE), :] = nr + ncol[4 * sup + a:4 * sup + a + 1, :] - 2.0 * tile
                begin([rs_copy(st, 0, 2 * u), rs_copy(st, 0, 2 * u + 1)])

        def row_sums(st, k, kern):
            place = own(0, k) - base(0, k)
            slot, r = div(place, TILE), rem(place, TILE)

            def by_rows(vals):
                rs = jnp.sum(vals, axis=1, keepdims=True)
                return jnp.sum(jnp.where(lane_o == sub_o + r, rs, 0.0), axis=0, keepdims=True)

            def by_cols(vals):
                return jnp.sum(vals, axis=0, keepdims=True)

            if st > 0:
                sup, m = UNITS[st][k // 2]
                return [(4 * m + 2 * core + k % 2, by_rows(kern)), (4 * sup + slot, by_cols(kern))]
            both = div(slot, 3)
            i0 = (1 - both) * core * (1 + div(slot, 2)) + both * 2 * core
            j0 = (1 - both) * ((1 - core) * (slot + 1) + core * (2 + div(slot + 1, 2))) + both * 2 * core
            up = jnp.where(lane_o + 1000 * (1 - both) > sub_o + r, kern, 0.0)
            lo = jnp.where(lane_o + 1000 * (1 - both) < sub_o + r, kern, 0.0)
            nxt = 4 * k + 2 * core + 1
            return [(4 * k + i0, by_rows(up)), (4 * k + j0, by_cols(up)), (nxt, by_rows(lo)), (nxt, by_cols(lo))]

        def advance(st, s):
            parts = [[], [], []]
            for k in range(COLORS):
                mine = pl.ds(al(own(st, k)), OWN)
                if s < 2:
                    peer, length, keep, give = halves[k][s]
                    rs_copy(st, s, k).wait_recv()
                    rng = pl.ds(al(base(st, k) + keep), length)
                    pack[rng, :] += (r0, r1)[s][st, k]
                    begin([rs_copy(st, 1, k)] if s == 0 else x_copies(st, 0, k))
                elif s == 2:
                    x_arrive(st, 0, k)
                    r3[st, k, coords[dims(k)[2]]] = pack[mine, :] + r2[st, k, 0] + r2[st, k, 1] + r2[st, k, 2]
                    begin(x_copies(st, 1, k))
                elif s == 3:
                    x_arrive(st, 1, k)
                    full = (r3[st, k, 0] + r3[st, k, 1]) + (r3[st, k, 2] + r3[st, k, 3])
                    if st == 0 and k >= 4:
                        kern = full
                    else:
                        kern = jnp.exp(-jnp.maximum(full, 0.0) / bandwidth)
                        parts[k % 3] += row_sums(st, k, kern)
                    kg[core, mine, :] = kern.astype(BF16)
                    begin(x_copies(st, 2, k))
                elif s == 4:
                    x_arrive(st, 2, k)
                    begin(x_copies(st, 3, k))
                    begin([dd_copy(st, k, 0)])
                else:
                    for j, cp in enumerate(x_copies(st, 3, k)):
                        cp.wait_recv()
                        begin([dd_copy(st, k, j + 1)])
            if s == 3:
                for d in range(3):
                    svec[st, 0, d] = jnp.zeros((16, TILE), F32)
                    for block, line in parts[d]:
                        svec[st, 0, d, pl.ds(block, 1), :] += line
                    begin(s_copies(st, 0, d))
            if s == 4:
                for d in range(3):
                    arrive(srecv.at[st, 0, d], s_recv.at[st, 0, d])
                    svec[st, 1, d] = svec[st, 0, d] + srecv[st, 0, d, 0] + srecv[st, 0, d, 1] + srecv[st, 0, d, 2]
                    begin(s_copies(st, 1, d))
            if s == 5:
                tot = jnp.zeros((16, TILE), F32)
                for d in range(3):
                    arrive(srecv.at[st, 1, d], s_recv.at[st, 1, d])
                    tot = tot + ((svec[st, 1, d] + srecv[st, 1, d, 0]) + (srecv[st, 1, d, 1] + srecv[st, 1, d, 2]))
                stot[st] = tot
                begin([sp_copy(st)])

        def unpack(st):
            for k in range(COLORS):
                arrive(kg.at[core, 0:BLK], dd_recv.at[st, k])
            for c in range(2):
                if st > 0:
                    for k in range(COLORS):
                        sup, m = UNITS[st][k // 2]
                        jrng = pl.ds((4 * m + 2 * c + k % 2) * TILE, TILE)
                        for a in range(4):
                            src = kg[c, pl.ds(base(st, k) + a * TILE, TILE), :]
                            srng = pl.ds((4 * sup + a) * TILE, TILE)
                            kfull[jrng, srng] = src
                            kfull[srng, jrng] = src.T
                    continue
                for sup in range(4):
                    for t, (i, j) in enumerate(OFFS[c]):
                        src = kg[c, pl.ds(base(0, sup) + t * TILE, TILE), :]
                        ri, rj = pl.ds((4 * sup + i) * TILE, TILE), pl.ds((4 * sup + j) * TILE, TILE)
                        kfull[ri, rj] = src
                        kfull[rj, ri] = src.T
                    src = kg[c, pl.ds(base(0, sup) + 3 * TILE, TILE), :]
                    srt = src.T
                    one = jnp.ones((TILE, TILE), BF16)
                    ra, rb = pl.ds((4 * sup + 2 * c) * TILE, TILE), pl.ds((4 * sup + 2 * c + 1) * TILE, TILE)
                    kfull[ra, ra] = jnp.where(upper, src, jnp.where(lower, srt, one))
                    kfull[rb, rb] = jnp.where(lower, src, jnp.where(upper, srt, one))

        def drive():
            for q in range(8):
                rows = pl.ds(q * 256, 256)
                pm = kg[q % 2, pl.ds(PM_ROW + (q // 2) * 256, 256), :]
                low = lax.dot_general(pm, fac_ref[...], NT, preferred_element_type=F32)
                th = out_ref[rows, :]
                grad = -((th - mu_ref[...]) * lam_ref[...] + low)
                adrv[rows, :] = (grad - rep_coef * th).astype(BF16)

        def sum_rows(blocks):
            tot = stot[0] + spart[0] + stot[1] + spart[1] + 1.0
            if len(blocks) > 4:
                tot = tot + (stot[2] + spart[2])
            for blk in blocks:
                line = jnp.sum(jnp.where(eye, jnp.broadcast_to(tot[blk:blk + 1, :], (TILE, TILE)), 0.0), axis=1, keepdims=True)
                srow[pl.ds(blk * TILE, TILE), :] = jnp.broadcast_to(rep_coef * line, (TILE, TILE))

        def update(ch):
            for half in range(2):
                start = ch * BLK + half * 256
                rows = pl.ds(start, 256)
                acc = jnp.dot(kfull[rows, :], adrv[...], preferred_element_type=F32)
                new = []
                for t in range(width // TILE):
                    cols = slice(t * TILE, (t + 1) * TILE)
                    th = out_ref[rows, cols]
                    phi = (acc[:, cols] + srow[rows, :] * th) / n_part
                    new.append(th + step_size * phi)
                th = jnp.concatenate(new, axis=1)
                out_ref[rows, :] = th
                prepare(start, 256, th)
            begin([pre_copy(ch, 1), pre_copy(ch, 0)])

        unit_tiles(1, (0, 1, 2))
        unit_tiles(2, (0, 1))
        unit_tiles(2, (2,))
        for s in range(5):
            for st in range(3):
                advance(st, s)
        advance(0, 5)
        advance(1, 5)
        unpack(0)
        drive()
        advance(2, 5)
        remote(pack.at[0:5120], pack.at[0:5120], pre_send, sp_recv.at[0], mate).wait_send()
        for st in range(2):
            arrive(stot.at[st], sp_recv.at[st])
        sum_rows(range(4))
        unpack(1)
        update(0)
        arrive(stot.at[2], sp_recv.at[2])
        sum_rows(range(4, 16))
        unpack(2)
        for ch in range(1, 4):
            update(ch)
        for st in range(3):
            remote(pack.at[0:SENT], pack.at[0:SENT], sent.at[st], sp_recv.at[0], mate).wait_send()
        pl.when(step_index < NUM_STEPS - 1)(open_step)
        return carry

    lax.fori_loop(0, NUM_STEPS, one_step, 0)
    for ch in range(4):
        for what in range(2):
            pre_copy(ch, what).wait_recv()
    remote(pack.at[0:5120], pack.at[0:5120], pre_send, sp_recv.at[0], mate).wait_send()


def solution(mesh):
    def run_steps(particles, prec_diag, mean_vec, low_rank):
        total_rows, width = particles.shape
        n_part = total_rows // mesh.shape["ens"]
        bandwidth = BAND_SCALE * width
        step_size = STEP_SCALE * width
        loc = width // (mesh.shape["slab"] * mesh.shape["feat"])
        rank = low_rank.shape[1]
        vm, dma = pltpu.VMEM, pltpu.SemaphoreType.DMA

        def local_steps(current, prec_loc, mean_loc, fac_loc):
            spec = pl.BlockSpec(memory_space=pltpu.VMEM)
            call = pl.pallas_call(
                functools.partial(_kernel, bandwidth, step_size, n_part),
                out_shape=jax.ShapeDtypeStruct((n_part, loc), F32),
                in_specs=[pl.BlockSpec(memory_space=pltpu.HBM)] + [spec] * 3,
                out_specs=spec,
                scratch_shapes=[
                    vm((ROWS, 2 * loc), BF16), vm((ROWS, rank), F32), vm((ROWS // 2, rank), F32),
                    vm((ROWS, TILE), F32), vm((16, TILE), F32), vm((ROWS, TILE), F32),
                    vm((3 * SROWS, TILE), F32),
                    vm((3, COLORS, BLK // 2, TILE), F32), vm((3, COLORS, BLK // 4, TILE), F32),
                    vm((3, COLORS, 3, OWN, TILE), F32), vm((3, COLORS, 4, OWN, TILE), F32),
                    vm((2, 3 * SROWS, TILE), BF16), vm((ROWS, ROWS), BF16), vm((ROWS, loc), BF16),
                    vm((3, 2, 3, 16, TILE), F32), vm((3, 2, 3, 3, 16, TILE), F32), vm((3, 16, TILE), F32), vm((3, 16, TILE), F32),
                    dma((4,)), dma, dma((2, 4)), dma((3,)), dma((3, 2, COLORS)), dma((3, 3, COLORS)), dma((3, COLORS, 3)), dma((3, COLORS)),
                    dma((3, 2, 3)), dma((3,)),
                ],
                compiler_params=pltpu.CompilerParams(collective_id=0, has_side_effects=True, vmem_limit_bytes=48 * 1024 * 1024),
                name="svgd",
            )
            return call(current, prec_loc.reshape(1, loc), mean_loc.reshape(1, loc), fac_loc)

        sharded = jax.shard_map(
            local_steps,
            mesh=mesh,
            in_specs=(P("ens", FEAT_AXES), P(LEAD_AXES), P(LEAD_AXES), P(LEAD_AXES, None)),
            out_specs=P("ens", FEAT_AXES),
            check_vma=False,
        )
        return sharded(particles, prec_diag, mean_vec, low_rank)

    return run_steps
```

time: 176 us -> 162 us (0.920)
  Pallas kernels: 171 us -> 158 us
    pallas_call x1, Pallas kernels: 171 us -> 158 us  [local_steps(): call(current, prec_loc.reshape(1, loc), mean_loc.reshape(1, loc), fac_loc)]
    unnamed x1 -> x7, local copies, waits for them, and re-layouts: 4.64 us -> 4.28 us
where the time goes in v2:
time: 162 us
  Pallas kernels  158 us (98%)
  local copies, waits for them, and re-layouts  4.28 us (3%)
    pallas_call x1, Pallas kernels, local_steps(): call(current, prec_loc.reshape(1, loc), mean_loc.reshape(1, loc), fac_loc)  158 us
    unnamed x7, local copies, waits for them, and re-layouts  4.28 us

profile of v2, /device:TPU:1, one launch (start us, length us, event | category | flops | bytes accessed | tf_op | source)
XLA Modules:
  0.0 161.9 jit_solution(12286957500825100850)
XLA Ops:
  0.0 0.0 copy-start
  0.0 0.9 copy-done
  0.9 0.0 copy-start.1
  0.9 0.7 copy-done.1
  1.6 0.0 copy-start.2
  1.6 0.7 copy-done.2
  2.3 157.6 %svgd.1 = f32[2048,512]{1,0:T(8,128)S(1)} custom-call(f32[2048,512]{1,0:T(8,128)} %theta_ref.1, f32[1,512]{1,0:T(1,128)S(1)} %bitcast.2, f32[1,512]{1,0:T(1,128)S(1)} %bitcast.3, bf16[512,128]{1,0:T(8,128)(2,1)S(1)} %copy-done), custom_call_target="tpu_custom_call" | custom-call | tf_op jit(solution)/shard_map/svgd/pallas_call | solution.py:446
  159.9 2.0 %copy.6 = f32[2048,512]{1,0:T(8,128)} copy(f32[2048,512]{1,0:T(8,128)S(1)} %svgd.1) | data formatting | bytes 8388608
Async XLA Ops:
  0.0 0.9 copy-start
  0.9 0.7 copy-start.1
  1.6 0.7 copy-start.2

commit v3 on v2

--- a/solution.py
+++ b/solution.py
@@ -18,8 +18,8 @@
 BLK = 512
 COLORS = 6
 SROWS = COLORS * BLK
-UNITS = (None, ((0, 1), (0, 2), (0, 3)), ((1, 2), (1, 3), (2, 3)))
-OFFS = (((0, 1), (0, 2), (0, 3)), ((1, 2), (1, 3), (2, 3)))
+UNITS = ((), ((0, 3), (0, 1), (0, 2)), ((1, 2), (1, 3), (2, 3)))
+OFFS = (((0, 1), (2, 0), (3, 0)), ((1, 2), (1, 3), (2, 3)))
 PM_ROW = 4 * BLK
 SENT = 1536 + 768 + 576 + 576 + 288 + 1152 + 1536 + 288 + 16
 OWN = 32
@@ -38,7 +38,8 @@
 
 def _kernel(
     bandwidth, step_size, n_part,
-    theta_ref, lam_ref, mu_ref, fac_ref, out_ref,
+    theta_ref, lam_hbm, mu_hbm, fac_hbm, out_ref,
+    lam_ref, mu_ref, fac_ref,
     bfull, pml, pmr, nrow, ncol, srow, pack, r0, r1, r2, r3, kg, kfull, adrv, svec, srecv, stot, spart,
     in_sem, pre_send, pre_recv, sent, rs_recv, x_recv, far_recv, dd_recv, s_recv, sp_recv,
 ):
@@ -109,7 +110,11 @@
         for j in range(1, 4):
             pl.semaphore_signal(barrier, inc=1, device_id=ring[dim][j], device_id_type=MESH)
     loads = [pltpu.make_async_copy(theta_ref.at[pl.ds(ch * BLK, BLK)], out_ref.at[pl.ds(ch * BLK, BLK)], in_sem.at[ch]) for ch in range(4)]
-    for cp in loads:
+    loads += [
+        pltpu.make_async_copy(src, dst, in_sem.at[4 + n])
+        for n, (src, dst) in enumerate(((mu_hbm, mu_ref), (fac_hbm, fac_ref), (lam_hbm, lam_ref)))
+    ]
+    for cp in loads[4:] + loads[:4]:
         cp.start()
 
     row_i = lax.broadcasted_iota(jnp.int32, (TILE, TILE), 0)
@@ -184,29 +189,43 @@
     def sp_copy(st):
         return remote(stot.at[st], spart.at[st], sent.at[st], sp_recv.at[st], mate)
 
-    def diag_tiles(sup):
-        bb = bfull[pl.ds(sup * BLK, BLK), :]
-        g = lax.dot_general(bb, bb, NT, preferred_element_type=F32)
-
-        def tile(i, j):
-            return g[i * TILE:(i + 1) * TILE, j * TILE:(j + 1) * TILE]
-
-        rows_n, cols_n = [], []
-        for i in range(4):
-            d = jnp.where(eye, tile(i, i), 0.0)
-            rows_n.append(jnp.broadcast_to(jnp.sum(d, axis=1, keepdims=True), (TILE, TILE)))
-            cols_n.append(jnp.sum(d, axis=0, keepdims=True))
-            nrow[pl.ds((4 * sup + i) * TILE, TILE), :] = rows_n[i]
-            ncol[pl.ds(4 * sup + i, 1), :] = cols_n[i]
+    def products(m):
+        mine = bfull[pl.ds(al(m * BLK + 256 * core), 256), :]
+        other = bfull[pl.ds(al(m * BLK + 256 * (1 - core)), 256), :]
+        g = lax.dot_general(bfull[pl.ds(0, (m + 1) * BLK), :], mine, NT, preferred_element_type=F32)
+        return g, lax.dot_general(other, other, NT, preferred_element_type=F32)
+
+    def tiles(m, g, g_other):
+        def tile(i, b):
+            return g[m * BLK + i * TILE:m * BLK + (i + 1) * TILE, b * TILE:(b + 1) * TILE]
+
+        for b in range(2):
+            own_diag = jnp.where(core == 0, tile(b, b), tile(2 + b, b))
+            rng = slice(b * TILE, (b + 1) * TILE)
+            for half, diag in ((core, own_diag), (1 - core, g_other[rng, rng])):
+                d = jnp.where(eye, diag, 0.0)
+                blk = 4 * m + 2 * half + b
+                nrow[pl.ds(al(blk * TILE), TILE), :] = jnp.broadcast_to(jnp.sum(d, axis=1, keepdims=True), (TILE, TILE))
+                ncol[pl.ds(blk, 1), :] = jnp.sum(d, axis=0, keepdims=True)
 
         def dist(i, j):
-            return rows_n[i] + cols_n[j] - 2.0 * tile(i, j)
+            return nrow[pl.ds((4 * m + i) * TILE, TILE), :] + ncol[4 * m + j:4 * m + j + 1, :] - 2.0 * tile(i, j % 2)
 
         for t in range(3):
-            pack[pl.ds(base(0, sup) + t * TILE, TILE), :] = jnp.where(core == 0, dist(*OFFS[0][t]), dist(*OFFS[1][t]))
+            pack[pl.ds(base(0, m) + t * TILE, TILE), :] = jnp.where(core == 0, dist(*OFFS[0][t]), dist(*OFFS[1][t]))
         one = jnp.where(core == 0, dist(0, 0), dist(2, 2))
         two = jnp.where(core == 0, dist(1, 1), dist(3, 3))
-        pack[pl.ds(base(0, sup) + 3 * TILE, TILE), :] = jnp.where(upper, one, two)
+        pack[pl.ds(base(0, m) + 3 * TILE, TILE), :] = jnp.where(upper, one, two)
+        begin([rs_copy(0, 0, m)])
+        for st in (1, 2):
+            for u, (sup, col) in enumerate(UNITS[st]):
+                if col != m:
+                    continue
+                for b in range(2):
+                    nc = ncol[pl.ds(4 * m + 2 * core + b, 1), :]
+                    part = g[sup * BLK:(sup + 1) * BLK, b * TILE:(b + 1) * TILE]
+                    pack[pl.ds(base(st, 2 * u + b), BLK), :] = nrow[pl.ds(sup * BLK, BLK), :] + nc - 2.0 * part
+                begin([rs_copy(st, 0, 2 * u), rs_copy(st, 0, 2 * u + 1)])
 
     def pm_tiles():
         for ch in range(4):
@@ -216,13 +235,19 @@
         begin([rs_copy(0, 0, 4), rs_copy(0, 0, 5)])
 
     def open_step():
-        for sup in range(4):
-            pre_copy(sup, 0).wait_recv()
-            diag_tiles(sup)
-            begin([rs_copy(0, 0, sup)])
-            if sup == 2:
+        for ch in range(3):
+            pre_copy(ch, 0).wait_recv()
+        gs = [products(0)]
+        for m in range(4):
+            if m == 2:
                 pm_tiles()
-
+                pre_copy(3, 0).wait_recv()
+            if m < 3:
+                gs.append(products(m + 1))
+            tiles(m, *gs[m])
+
+    for cp in loads[4:]:
+        cp.wait()
     for ch in range(4):
         loads[ch].wait()
         prepare(ch * BLK, BLK, out_ref[pl.ds(ch * BLK, BLK), :])
@@ -232,19 +257,6 @@
     open_step()
 
     def one_step(step_index, carry):
-        def unit_tiles(st, units):
-            sup = UNITS[st][units[0]][0]
-            blocks = [4 * UNITS[st][u][1] + 2 * core for u in units]
-            lhs = jnp.concatenate([bfull[pl.ds(al(blk * TILE), 256), :] for blk in blocks], axis=0)
-            g = lax.dot_general(lhs, bfull[pl.ds(sup * BLK, BLK), :], NT, preferred_element_type=F32)
-            for n, u in enumerate(units):
-                for b in range(2):
-                    nr = nrow[pl.ds(al((blocks[n] + b) * TILE), TILE), :]
-                    for a in range(4):
-                        tile = g[n * 256 + b * TILE:n * 256 + (b + 1) * TILE, a * TILE:(a + 1) * TILE]
-                        pack[pl.ds(base(st, 2 * u + b) + a * TILE, TILE), :] = nr + ncol[4 * sup + a:4 * sup + a + 1, :] - 2.0 * tile
-                begin([rs_copy(st, 0, 2 * u), rs_copy(st, 0, 2 * u + 1)])
-
         def row_sums(st, k, kern):
             place = own(0, k) - base(0, k)
             slot, r = div(place, TILE), rem(place, TILE)
@@ -258,10 +270,11 @@
 
             if st > 0:
                 sup, m = UNITS[st][k // 2]
-                return [(4 * m + 2 * core + k % 2, by_rows(kern)), (4 * sup + slot, by_cols(kern))]
+                return [(4 * sup + slot, by_rows(kern)), (4 * m + 2 * core + k % 2, by_cols(kern))]
             both = div(slot, 3)
-            i0 = (1 - both) * core * (1 + div(slot, 2)) + both * 2 * core
-            j0 = (1 - both) * ((1 - core) * (slot + 1) + core * (2 + div(slot + 1, 2))) + both * 2 * core
+            up_one = div(slot + 1, 2)
+            i0 = (1 - both) * ((1 - core) * (slot + up_one) + core * (1 + div(slot, 2))) + both * 2 * core
+            j0 = (1 - both) * ((1 - core) * (1 - up_one) + core * (2 + up_one)) + both * 2 * core
             up = jnp.where(lane_o + 1000 * (1 - both) > sub_o + r, kern, 0.0)
             lo = jnp.where(lane_o + 1000 * (1 - both) < sub_o + r, kern, 0.0)
             nxt = 4 * k + 2 * core + 1
@@ -329,8 +342,8 @@
                         for a in range(4):
                             src = kg[c, pl.ds(base(st, k) + a * TILE, TILE), :]
                             srng = pl.ds((4 * sup + a) * TILE, TILE)
-                            kfull[jrng, srng] = src
-                            kfull[srng, jrng] = src.T
+                            kfull[srng, jrng] = src
+                            kfull[jrng, srng] = src.T
                     continue
                 for sup in range(4):
                     for t, (i, j) in enumerate(OFFS[c]):
@@ -362,11 +375,18 @@
                 line = jnp.sum(jnp.where(eye, jnp.broadcast_to(tot[blk:blk + 1, :], (TILE, TILE)), 0.0), axis=1, keepdims=True)
                 srow[pl.ds(blk * TILE, TILE), :] = jnp.broadcast_to(rep_coef * line, (TILE, TILE))
 
-        def update(ch):
-            for half in range(2):
-                start = ch * BLK + half * 256
+        def update(chs):
+            starts = [ch * BLK + half * 256 for ch in chs for half in range(2)]
+
+            def product(start):
+                return jnp.dot(kfull[pl.ds(start, 256), :], adrv[...], preferred_element_type=F32)
+
+            ahead = product(starts[0])
+            for n, start in enumerate(starts):
+                acc = ahead
+                if n + 1 < len(starts):
+                    ahead = product(starts[n + 1])
                 rows = pl.ds(start, 256)
-                acc = jnp.dot(kfull[rows, :], adrv[...], preferred_element_type=F32)
                 new = []
                 for t in range(width // TILE):
                     cols = slice(t * TILE, (t + 1) * TILE)
@@ -376,11 +396,9 @@
                 th = jnp.concatenate(new, axis=1)
                 out_ref[rows, :] = th
                 prepare(start, 256, th)
-            begin([pre_copy(ch, 1), pre_copy(ch, 0)])
-
-        unit_tiles(1, (0, 1, 2))
-        unit_tiles(2, (0, 1))
-        unit_tiles(2, (2,))
+                if n % 2 == 1:
+                    begin([pre_copy(chs[n // 2], 1), pre_copy(chs[n // 2], 0)])
+
         for s in range(5):
             for st in range(3):
                 advance(st, s)
@@ -394,12 +412,11 @@
             arrive(stot.at[st], sp_recv.at[st])
         sum_rows(range(4))
         unpack(1)
-        update(0)
+        update((0,))
         arrive(stot.at[2], sp_recv.at[2])
         sum_rows(range(4, 16))
         unpack(2)
-        for ch in range(1, 4):
-            update(ch)
+        update((1, 2, 3))
         for st in range(3):
             remote(pack.at[0:SENT], pack.at[0:SENT], sent.at[st], sp_recv.at[0], mate).wait_send()
         pl.when(step_index < NUM_STEPS - 1)(open_step)
@@ -427,9 +444,10 @@
             call = pl.pallas_call(
                 functools.partial(_kernel, bandwidth, step_size, n_part),
                 out_shape=jax.ShapeDtypeStruct((n_part, loc), F32),
-                in_specs=[pl.BlockSpec(memory_space=pltpu.HBM)] + [spec] * 3,
+                in_specs=[pl.BlockSpec(memory_space=pltpu.HBM)] * 4,
                 out_specs=spec,
                 scratch_shapes=[
+                    vm((1, loc), F32), vm((1, loc), F32), vm((loc, rank), BF16),
                     vm((ROWS, 2 * loc), BF16), vm((ROWS, rank), F32), vm((ROWS // 2, rank), F32),
                     vm((ROWS, TILE), F32), vm((16, TILE), F32), vm((ROWS, TILE), F32),
                     vm((3 * SROWS, TILE), F32),
@@ -437,13 +455,14 @@
                     vm((3, COLORS, 3, OWN, TILE), F32), vm((3, COLORS, 4, OWN, TILE), F32),
                     vm((2, 3 * SROWS, TILE), BF16), vm((ROWS, ROWS), BF16), vm((ROWS, loc), BF16),
                     vm((3, 2, 3, 16, TILE), F32), vm((3, 2, 3, 3, 16, TILE), F32), vm((3, 16, TILE), F32), vm((3, 16, TILE), F32),
-                    dma((4,)), dma, dma((2, 4)), dma((3,)), dma((3, 2, COLORS)), dma((3, 3, COLORS)), dma((3, COLORS, 3)), dma((3, COLORS)),
+                    dma((7,)), dma, dma((2, 4)), dma((3,)), dma((3, 2, COLORS)), dma((3, 3, COLORS)), dma((3, COLORS, 3)), dma((3, COLORS)),
                     dma((3, 2, 3)), dma((3,)),
                 ],
-                compiler_params=pltpu.CompilerParams(collective_id=0, has_side_effects=True, vmem_limit_bytes=48 * 1024 * 1024),
+                compiler_params=pltpu.CompilerParams(collective_id=0, has_side_effects=True, vmem_limit_bytes=50000000),
                 name="svgd",
             )
-            return call(current, prec_loc.reshape(1, loc), mean_loc.reshape(1, loc), fac_loc)
+            hbm = lambda x: pltpu.with_memory_space_constraint(x, pltpu.HBM)
+            return call(hbm(current), hbm(prec_loc.reshape(1, loc)), hbm(mean_loc.reshape(1, loc)), hbm(fac_loc))
 
         sharded = jax.shard_map(
             local_steps,

time: 162 us -> 162 us (level)
  local copies, waits for them, and re-layouts: 4.28 us -> 2.02 us
  Pallas kernels: 158 us -> 160 us
    unnamed x7 -> x1, local copies, waits for them, and re-layouts: 4.28 us -> 2.02 us
    pallas_call x1, Pallas kernels: 158 us -> 160 us  [local_steps(): call(hbm(current), hbm(prec_loc.reshape(1, loc)), hbm(mean_loc.reshape(1,...]
where the time goes in v3:
time: 162 us
  Pallas kernels  160 us (99%)
  local copies, waits for them, and re-layouts  2.02 us (1%)
    pallas_call x1, Pallas kernels, local_steps(): call(hbm(current), hbm(prec_loc.reshape(1, loc)), hbm(mean_loc.reshape(1,...  160 us

profile of v3, /device:TPU:1, one launch (start us, length us, event | category | flops | bytes accessed | tf_op | source)
XLA Modules:
  0.0 161.6 jit_solution(6246483150294913389)
XLA Ops:
  0.0 159.6 %svgd.1 = f32[2048,512]{1,0:T(8,128)S(1)} custom-call(f32[2048,512]{1,0:T(8,128)} %theta_ref.1, f32[1,512]{1,0:T(1,128)} %bitcast.2, f32[1,512]{1,0:T(1,128)} %bitcast.3, bf16[512,128]{1,0:T(8,128)(2,1)} %fac_hbm.1), custom_call_target="tpu_custom_call" | custom-call | tf_op jit(solution)/shard_map/svgd/pallas_call | solution.py:465
  159.6 2.0 %copy.6 = f32[2048,512]{1,0:T(8,128)} copy(f32[2048,512]{1,0:T(8,128)S(1)} %svgd.1) | data formatting | bytes 8388608

commit v4 on v3

--- a/solution.py
+++ b/solution.py
@@ -21,7 +21,8 @@
 UNITS = ((), ((0, 3), (0, 1), (0, 2)), ((1, 2), (1, 3), (2, 3)))
 OFFS = (((0, 1), (2, 0), (3, 0)), ((1, 2), (1, 3), (2, 3)))
 PM_ROW = 4 * BLK
-SENT = 1536 + 768 + 576 + 576 + 288 + 1152 + 1536 + 288 + 16
+SENT = 1536 + 768 + 576 + 576 + 288 + 1152 + 1536
+SENT_SUMS = 288 + 16
 OWN = 32
 MESH = pl.DeviceIdType.MESH
 NT = (((1,), (1,)), ((), ()))
@@ -179,34 +180,36 @@
         rng = pl.ds(al(begin_row), TILE)
         return remote(kg.at[core, rng], kg.at[core, rng], sent.at[st], dd_recv.at[st, k], mate)
 
-    def s_copies(st, ph, d):
+    def s_copies(ph, d):
         dim = ((d + 1) % 3, d)[ph]
         return [
-            remote(svec.at[st, ph, d], srecv.at[st, ph, d, j - 1], sent.at[st], s_recv.at[st, ph, d], ring[dim][j])
+            remote(svec.at[ph, d], srecv.at[ph, d, j - 1], sent.at[2], s_recv.at[ph, d], ring[dim][j])
             for j in range(1, 4)
         ]
 
-    def sp_copy(st):
-        return remote(stot.at[st], spart.at[st], sent.at[st], sp_recv.at[st], mate)
+    def sp_copy():
+        return remote(stot, spart, sent.at[2], sp_recv, mate)
 
     def products(m):
         mine = bfull[pl.ds(al(m * BLK + 256 * core), 256), :]
-        other = bfull[pl.ds(al(m * BLK + 256 * (1 - core)), 256), :]
-        g = lax.dot_general(bfull[pl.ds(0, (m + 1) * BLK), :], mine, NT, preferred_element_type=F32)
-        return g, lax.dot_general(other, other, NT, preferred_element_type=F32)
-
-    def tiles(m, g, g_other):
+        part = BLK if m == 3 else (m + 1) * 256
+        return [lax.dot_general(bfull[pl.ds(at, part), :], mine, NT, preferred_element_type=F32) for at in range(0, (m + 1) * BLK, part)]
+
+    def norms(m):
+        for i in range(4):
+            rows = pl.ds((4 * m + i) * TILE, TILE)
+            wide = bfull[rows, :].astype(F32)
+            n = jnp.broadcast_to(jnp.sum(wide * wide, axis=1, keepdims=True), (TILE, TILE))
+            nrow[rows, :] = n
+            ncol[4 * m + i:4 * m + i + 1, :] = jnp.sum(jnp.where(eye, n, 0.0), axis=0, keepdims=True)
+
+    def tiles(m, g):
+        def block(blk, b):
+            n, r = divmod(blk * TILE, BLK if m == 3 else (m + 1) * 256)
+            return g[n][r:r + TILE, b * TILE:(b + 1) * TILE]
+
         def tile(i, b):
-            return g[m * BLK + i * TILE:m * BLK + (i + 1) * TILE, b * TILE:(b + 1) * TILE]
-
-        for b in range(2):
-            own_diag = jnp.where(core == 0, tile(b, b), tile(2 + b, b))
-            rng = slice(b * TILE, (b + 1) * TILE)
-            for half, diag in ((core, own_diag), (1 - core, g_other[rng, rng])):
-                d = jnp.where(eye, diag, 0.0)
-                blk = 4 * m + 2 * half + b
-                nrow[pl.ds(al(blk * TILE), TILE), :] = jnp.broadcast_to(jnp.sum(d, axis=1, keepdims=True), (TILE, TILE))
-                ncol[pl.ds(blk, 1), :] = jnp.sum(d, axis=0, keepdims=True)
+            return block(4 * m + i, b)
 
         def dist(i, j):
             return nrow[pl.ds((4 * m + i) * TILE, TILE), :] + ncol[4 * m + j:4 * m + j + 1, :] - 2.0 * tile(i, j % 2)
@@ -223,8 +226,9 @@
                     continue
                 for b in range(2):
                     nc = ncol[pl.ds(4 * m + 2 * core + b, 1), :]
-                    part = g[sup * BLK:(sup + 1) * BLK, b * TILE:(b + 1) * TILE]
-                    pack[pl.ds(base(st, 2 * u + b), BLK), :] = nrow[pl.ds(sup * BLK, BLK), :] + nc - 2.0 * part
+                    for a in range(4):
+                        nr = nrow[pl.ds((4 * sup + a) * TILE, TILE), :]
+                        pack[pl.ds(base(st, 2 * u + b) + a * TILE, TILE), :] = nr + nc - 2.0 * block(4 * sup + a, b)
                 begin([rs_copy(st, 0, 2 * u), rs_copy(st, 0, 2 * u + 1)])
 
     def pm_tiles():
@@ -238,13 +242,15 @@
         for ch in range(3):
             pre_copy(ch, 0).wait_recv()
         gs = [products(0)]
+        norms(0)
         for m in range(4):
             if m == 2:
                 pm_tiles()
                 pre_copy(3, 0).wait_recv()
             if m < 3:
                 gs.append(products(m + 1))
-            tiles(m, *gs[m])
+                norms(m + 1)
+            tiles(m, gs[m])
 
     for cp in loads[4:]:
         cp.wait()
@@ -314,22 +320,24 @@
                         begin([dd_copy(st, k, j + 1)])
             if s == 3:
                 for d in range(3):
-                    svec[st, 0, d] = jnp.zeros((16, TILE), F32)
+                    if st == 0:
+                        svec[0, d] = jnp.zeros((16, TILE), F32)
                     for block, line in parts[d]:
-                        svec[st, 0, d, pl.ds(block, 1), :] += line
-                    begin(s_copies(st, 0, d))
-            if s == 4:
+                        svec[0, d, pl.ds(block, 1), :] += line
+                    if st == 2:
+                        begin(s_copies(0, d))
+            if st == 2 and s == 4:
                 for d in range(3):
-                    arrive(srecv.at[st, 0, d], s_recv.at[st, 0, d])
-                    svec[st, 1, d] = svec[st, 0, d] + srecv[st, 0, d, 0] + srecv[st, 0, d, 1] + srecv[st, 0, d, 2]
-                    begin(s_copies(st, 1, d))
-            if s == 5:
+                    arrive(srecv.at[0, d], s_recv.at[0, d])
+                    svec[1, d] = svec[0, d] + srecv[0, d, 0] + srecv[0, d, 1] + srecv[0, d, 2]
+                    begin(s_copies(1, d))
+            if st == 2 and s == 5:
                 tot = jnp.zeros((16, TILE), F32)
                 for d in range(3):
-                    arrive(srecv.at[st, 1, d], s_recv.at[st, 1, d])
-                    tot = tot + ((svec[st, 1, d] + srecv[st, 1, d, 0]) + (srecv[st, 1, d, 1] + srecv[st, 1, d, 2]))
-                stot[st] = tot
-                begin([sp_copy(st)])
+                    arrive(srecv.at[1, d], s_recv.at[1, d])
+                    tot = tot + ((svec[1, d] + srecv[1, d, 0]) + (srecv[1, d, 1] + srecv[1, d, 2]))
+                stot[...] = tot
+                begin([sp_copy()])
 
         def unpack(st):
             for k in range(COLORS):
@@ -367,11 +375,9 @@
                 grad = -((th - mu_ref[...]) * lam_ref[...] + low)
                 adrv[rows, :] = (grad - rep_coef * th).astype(BF16)
 
-        def sum_rows(blocks):
-            tot = stot[0] + spart[0] + stot[1] + spart[1] + 1.0
-            if len(blocks) > 4:
-                tot = tot + (stot[2] + spart[2])
-            for blk in blocks:
+        def sum_rows():
+            tot = stot[...] + spart[...] + 1.0
+            for blk in range(16):
                 line = jnp.sum(jnp.where(eye, jnp.broadcast_to(tot[blk:blk + 1, :], (TILE, TILE)), 0.0), axis=1, keepdims=True)
                 srow[pl.ds(blk * TILE, TILE), :] = jnp.broadcast_to(rep_coef * line, (TILE, TILE))
 
@@ -407,18 +413,16 @@
         unpack(0)
         drive()
         advance(2, 5)
-        remote(pack.at[0:5120], pack.at[0:5120], pre_send, sp_recv.at[0], mate).wait_send()
-        for st in range(2):
-            arrive(stot.at[st], sp_recv.at[st])
-        sum_rows(range(4))
+        remote(pack.at[0:5120], pack.at[0:5120], pre_send, sp_recv, mate).wait_send()
         unpack(1)
+        arrive(stot, sp_recv)
+        sum_rows()
         update((0,))
-        arrive(stot.at[2], sp_recv.at[2])
-        sum_rows(range(4, 16))
         unpack(2)
         update((1, 2, 3))
         for st in range(3):
-            remote(pack.at[0:SENT], pack.at[0:SENT], sent.at[st], sp_recv.at[0], mate).wait_send()
+            total = pack.at[0:SENT + (SENT_SUMS if st == 2 else 0)]
+            remote(total, total, sent.at[st], sp_recv, mate).wait_send()
         pl.when(step_index < NUM_STEPS - 1)(open_step)
         return carry
 
@@ -426,7 +430,7 @@
     for ch in range(4):
         for what in range(2):
             pre_copy(ch, what).wait_recv()
-    remote(pack.at[0:5120], pack.at[0:5120], pre_send, sp_recv.at[0], mate).wait_send()
+    remote(pack.at[0:5120], pack.at[0:5120], pre_send, sp_recv, mate).wait_send()
 
 
 def solution(mesh):
@@ -454,9 +458,9 @@
                     vm((3, COLORS, BLK // 2, TILE), F32), vm((3, COLORS, BLK // 4, TILE), F32),
                     vm((3, COLORS, 3, OWN, TILE), F32), vm((3, COLORS, 4, OWN, TILE), F32),
                     vm((2, 3 * SROWS, TILE), BF16), vm((ROWS, ROWS), BF16), vm((ROWS, loc), BF16),
-                    vm((3, 2, 3, 16, TILE), F32), vm((3, 2, 3, 3, 16, TILE), F32), vm((3, 16, TILE), F32), vm((3, 16, TILE), F32),
+                    vm((2, 3, 16, TILE), F32), vm((2, 3, 3, 16, TILE), F32), vm((16, TILE), F32), vm((16, TILE), F32),
                     dma((7,)), dma, dma((2, 4)), dma((3,)), dma((3, 2, COLORS)), dma((3, 3, COLORS)), dma((3, COLORS, 3)), dma((3, COLORS)),
-                    dma((3, 2, 3)), dma((3,)),
+                    dma((2, 3)), dma,
                 ],
                 compiler_params=pltpu.CompilerParams(collective_id=0, has_side_effects=True, vmem_limit_bytes=50000000),
                 name="svgd",

time: 162 us -> 158 us (0.975)
  Pallas kernels: 160 us -> 156 us
    pallas_call x1, Pallas kernels: 160 us -> 156 us  [local_steps(): call(hbm(current), hbm(prec_loc.reshape(1, loc)), hbm(mean_loc.reshape(1,...]
where the time goes in v4:
time: 158 us
  Pallas kernels  156 us (99%)
  local copies, waits for them, and re-layouts  2.02 us (1%)
    pallas_call x1, Pallas kernels, local_steps(): call(hbm(current), hbm(prec_loc.reshape(1, loc)), hbm(mean_loc.reshape(1,...  156 us

profile of v4, /device:TPU:1, one launch (start us, length us, event | category | flops | bytes accessed | tf_op | source)
XLA Modules:
  0.0 158.2 jit_solution(767263527529433772)
XLA Ops:
  0.0 156.1 %svgd.1 = f32[2048,512]{1,0:T(8,128)S(1)} custom-call(f32[2048,512]{1,0:T(8,128)} %theta_ref.1, f32[1,512]{1,0:T(1,128)} %bitcast.2, f32[1,512]{1,0:T(1,128)} %bitcast.3, bf16[512,128]{1,0:T(8,128)(2,1)} %fac_hbm.1), custom_call_target="tpu_custom_call" | custom-call | tf_op jit(solution)/shard_map/svgd/pallas_call | solution.py:469
  156.1 2.0 %copy.6 = f32[2048,512]{1,0:T(8,128)} copy(f32[2048,512]{1,0:T(8,128)S(1)} %svgd.1) | data formatting | bytes 8388608

commit v5 on v4

--- a/solution.py
+++ b/solution.py
@@ -41,7 +41,7 @@
     bandwidth, step_size, n_part,
     theta_ref, lam_hbm, mu_hbm, fac_hbm, out_ref,
     lam_ref, mu_ref, fac_ref,
-    bfull, pml, pmr, nrow, ncol, srow, pack, r0, r1, r2, r3, kg, kfull, adrv, svec, srecv, stot, spart,
+    bfull, pml, pmr, nrow, ncol, pack, r0, r1, r2, r3, kg, kfull, adrv, svec, srecv, stot, spart,
     in_sem, pre_send, pre_recv, sent, rs_recv, x_recv, far_recv, dd_recv, s_recv, sp_recv,
 ):
     width = out_ref.shape[1]
@@ -231,26 +231,24 @@
                         pack[pl.ds(base(st, 2 * u + b) + a * TILE, TILE), :] = nr + nc - 2.0 * block(4 * sup + a, b)
                 begin([rs_copy(st, 0, 2 * u), rs_copy(st, 0, 2 * u + 1)])
 
-    def pm_tiles():
-        for ch in range(4):
+    def pm_tiles(half):
+        for ch in (2 * half, 2 * half + 1):
             pre_copy(ch, 1).wait_recv()
             mine = pl.ds(al(ch * BLK + core * 256), 256)
             pack[pl.ds(PM_ROW + ch * 256, 256), :] = pml[mine, :] + pmr[pl.ds(ch * 256, 256), :]
-        begin([rs_copy(0, 0, 4), rs_copy(0, 0, 5)])
+        begin([rs_copy(0, 0, 4 + half)])
 
     def open_step():
-        for ch in range(3):
-            pre_copy(ch, 0).wait_recv()
-        gs = [products(0)]
-        norms(0)
-        for m in range(4):
-            if m == 2:
-                pm_tiles()
-                pre_copy(3, 0).wait_recv()
-            if m < 3:
-                gs.append(products(m + 1))
-                norms(m + 1)
-            tiles(m, gs[m])
+        for half in range(2):
+            pm_tiles(half)
+            gs = []
+            for m in (2 * half, 2 * half + 1):
+                pre_copy(m, 0).wait_recv()
+            for m in (2 * half, 2 * half + 1):
+                gs.append(products(m))
+                norms(m)
+            for n in range(2):
+                tiles(2 * half + n, gs[n])
 
     for cp in loads[4:]:
         cp.wait()
@@ -339,9 +337,11 @@
                 stot[...] = tot
                 begin([sp_copy()])
 
-        def unpack(st):
+        def unpack_wait(st):
             for k in range(COLORS):
                 arrive(kg.at[core, 0:BLK], dd_recv.at[st, k])
+
+        def unpack(st):
             for c in range(2):
                 if st > 0:
                     for k in range(COLORS):
@@ -375,29 +375,34 @@
                 grad = -((th - mu_ref[...]) * lam_ref[...] + low)
                 adrv[rows, :] = (grad - rep_coef * th).astype(BF16)
 
-        def sum_rows():
+        def product(start, cols):
+            return jnp.dot(kfull[pl.ds(start, 256), cols[0]:cols[1]], adrv[cols[0]:cols[1], :], preferred_element_type=F32)
+
+        def update(chs, early=()):
+            starts = [ch * BLK + half * 256 for ch in chs for half in range(2)]
             tot = stot[...] + spart[...] + 1.0
-            for blk in range(16):
-                line = jnp.sum(jnp.where(eye, jnp.broadcast_to(tot[blk:blk + 1, :], (TILE, TILE)), 0.0), axis=1, keepdims=True)
-                srow[pl.ds(blk * TILE, TILE), :] = jnp.broadcast_to(rep_coef * line, (TILE, TILE))
-
-        def update(chs):
-            starts = [ch * BLK + half * 256 for ch in chs for half in range(2)]
-
-            def product(start):
-                return jnp.dot(kfull[pl.ds(start, 256), :], adrv[...], preferred_element_type=F32)
-
-            ahead = product(starts[0])
+
+            def whole(n):
+                if n < len(early):
+                    return early[n] + product(starts[n], (2 * BLK, ROWS))
+                return product(starts[n], (0, ROWS))
+
+            ahead = whole(0)
             for n, start in enumerate(starts):
                 acc = ahead
                 if n + 1 < len(starts):
-                    ahead = product(starts[n + 1])
+                    ahead = whole(n + 1)
                 rows = pl.ds(start, 256)
+                sums = []
+                for blk in (start // TILE, start // TILE + 1):
+                    line = jnp.where(eye, jnp.broadcast_to(tot[blk:blk + 1, :], (TILE, TILE)), 0.0)
+                    sums.append(rep_coef * jnp.sum(line, axis=1, keepdims=True))
+                sums = jnp.broadcast_to(jnp.concatenate(sums, axis=0), (256, TILE))
                 new = []
                 for t in range(width // TILE):
                     cols = slice(t * TILE, (t + 1) * TILE)
                     th = out_ref[rows, cols]
-                    phi = (acc[:, cols] + srow[rows, :] * th) / n_part
+                    phi = (acc[:, cols] + sums * th) / n_part
                     new.append(th + step_size * phi)
                 th = jnp.concatenate(new, axis=1)
                 out_ref[rows, :] = th
@@ -410,16 +415,19 @@
                 advance(st, s)
         advance(0, 5)
         advance(1, 5)
+        unpack_wait(0)
         unpack(0)
         drive()
         advance(2, 5)
         remote(pack.at[0:5120], pack.at[0:5120], pre_send, sp_recv, mate).wait_send()
+        unpack_wait(1)
         unpack(1)
         arrive(stot, sp_recv)
-        sum_rows()
         update((0,))
+        unpack_wait(2)
+        early = [product(BLK + half * 256, (0, 2 * BLK)) for half in range(2)]
         unpack(2)
-        update((1, 2, 3))
+        update((1, 2, 3), early)
         for st in range(3):
             total = pack.at[0:SENT + (SENT_SUMS if st == 2 else 0)]
             remote(total, total, sent.at[st], sp_recv, mate).wait_send()
@@ -453,7 +461,7 @@
                 scratch_shapes=[
                     vm((1, loc), F32), vm((1, loc), F32), vm((loc, rank), BF16),
                     vm((ROWS, 2 * loc), BF16), vm((ROWS, rank), F32), vm((ROWS // 2, rank), F32),
-                    vm((ROWS, TILE), F32), vm((16, TILE), F32), vm((ROWS, TILE), F32),
+                    vm((ROWS, TILE), F32), vm((16, TILE), F32),
                     vm((3 * SROWS, TILE), F32),
                     vm((3, COLORS, BLK // 2, TILE), F32), vm((3, COLORS, BLK // 4, TILE), F32),
                     vm((3, COLORS, 3, OWN, TILE), F32), vm((3, COLORS, 4, OWN, TILE), F32),

time: 158 us -> 155 us (0.981)
  Pallas kernels: 156 us -> 153 us
    pallas_call x1, Pallas kernels: 156 us -> 153 us  [local_steps(): call(hbm(current), hbm(prec_loc.reshape(1, loc)), hbm(mean_loc.reshape(1,...]
where the time goes in v5:
time: 155 us
  Pallas kernels  153 us (99%)
  local copies, waits for them, and re-layouts  2.02 us (1%)
    pallas_call x1, Pallas kernels, local_steps(): call(hbm(current), hbm(prec_loc.reshape(1, loc)), hbm(mean_loc.reshape(1,...  153 us

profile of v5, /device:TPU:1, one launch (start us, length us, event | category | flops | bytes accessed | tf_op | source)
XLA Modules:
  0.0 155.2 jit_solution(11105357408455884999)
XLA Ops:
  0.0 153.2 %svgd.1 = f32[2048,512]{1,0:T(8,128)S(1)} custom-call(f32[2048,512]{1,0:T(8,128)} %theta_ref.1, f32[1,512]{1,0:T(1,128)} %bitcast.2, f32[1,512]{1,0:T(1,128)} %bitcast.3, bf16[512,128]{1,0:T(8,128)(2,1)} %fac_hbm.1), custom_call_target="tpu_custom_call" | custom-call | tf_op jit(solution)/shard_map/svgd/pallas_call | solution.py:477
  153.2 2.0 %copy.6 = f32[2048,512]{1,0:T(8,128)} copy(f32[2048,512]{1,0:T(8,128)S(1)} %svgd.1) | data formatting | bytes 8388608

commit v6 on v5

--- a/solution.py
+++ b/solution.py
@@ -155,6 +155,12 @@
         src = pack.at[pl.ds(al(base(st, k) + give), length)]
         return remote(src, (r0, r1)[s].at[st, k], sent.at[st], rs_recv.at[st, s, k], peer)
 
+    def gathered(st, k, row, rows):
+        if st == 0:
+            return kg.at[core, pl.ds(al(base(0, k) + row), rows)]
+        sup, m = UNITS[st][k // 2]
+        return kfull.at[pl.ds(al(sup * BLK + row), rows), pl.ds(al((4 * m + 2 * core + k % 2) * TILE, TILE), TILE)]
+
     def x_copies(st, e, k):
         d1, d2, d3 = dims(k)
         dim = (d2, d3, d2, d1)[e]
@@ -166,19 +172,15 @@
             elif e == 1:
                 src = dst = r3.at[st, k, coords[dim]]
             else:
-                rng = pl.ds(al(own(st, k)), OWN) if e == 2 else pl.ds(al(quarter(st, k)), TILE)
-                src = dst = kg.at[core, rng]
+                start = (own if e == 2 else quarter)(0, k) - base(0, k)
+                src = dst = gathered(st, k, start, OWN if e == 2 else TILE)
             arrived = far_recv.at[st, k, j - 1] if e == 3 else x_recv.at[st, e, k]
             cps.append(remote(src, dst, sent.at[st], arrived, ring[dim][j]))
         return cps
 
     def dd_copy(st, k, j):
-        if j == 0:
-            begin_row = quarter(st, k)
-        else:
-            begin_row = base(st, k) + places[k][4 - j]
-        rng = pl.ds(al(begin_row), TILE)
-        return remote(kg.at[core, rng], kg.at[core, rng], sent.at[st], dd_recv.at[st, k], mate)
+        ref = gathered(st, k, halves[k][1][2] if j == 0 else places[k][4 - j], TILE)
+        return remote(ref, ref, sent.at[st], dd_recv.at[st, k], mate)
 
     def s_copies(ph, d):
         dim = ((d + 1) % 3, d)[ph]
@@ -239,6 +241,7 @@
         begin([rs_copy(0, 0, 4 + half)])
 
     def open_step():
+        begin([pre_copy(3, 1), pre_copy(3, 0)])
         for half in range(2):
             pm_tiles(half)
             gs = []
@@ -256,7 +259,7 @@
         loads[ch].wait()
         prepare(ch * BLK, BLK, out_ref[pl.ds(ch * BLK, BLK), :])
     pl.semaphore_wait(barrier, 10)
-    for ch in range(4):
+    for ch in range(3):
         begin([pre_copy(ch, 1), pre_copy(ch, 0)])
     open_step()
 
@@ -286,6 +289,18 @@
 
         def advance(st, s):
             parts = [[], [], []]
+            if st == 2 and s == 4:
+                for d in range(3):
+                    arrive(srecv.at[0, d], s_recv.at[0, d])
+                    svec[1, d] = svec[0, d] + srecv[0, d, 0] + srecv[0, d, 1] + srecv[0, d, 2]
+                    begin(s_copies(1, d))
+            if st == 2 and s == 5:
+                tot = jnp.zeros((16, TILE), F32)
+                for d in range(3):
+                    arrive(srecv.at[1, d], s_recv.at[1, d])
+                    tot = tot + ((svec[1, d] + srecv[1, d, 0]) + (srecv[1, d, 1] + srecv[1, d, 2]))
+                stot[...] = tot
+                begin([sp_copy()])
             for k in range(COLORS):
                 mine = pl.ds(al(own(st, k)), OWN)
                 if s < 2:
@@ -306,7 +321,7 @@
                     else:
                         kern = jnp.exp(-jnp.maximum(full, 0.0) / bandwidth)
                         parts[k % 3] += row_sums(st, k, kern)
-                    kg[core, mine, :] = kern.astype(BF16)
+                    gathered(st, k, own(0, k) - base(0, k), OWN)[...] = kern.astype(BF16)
                     begin(x_copies(st, 2, k))
                 elif s == 4:
                     x_arrive(st, 2, k)
@@ -324,19 +339,6 @@
                         svec[0, d, pl.ds(block, 1), :] += line
                     if st == 2:
                         begin(s_copies(0, d))
-            if st == 2 and s == 4:
-                for d in range(3):
-                    arrive(srecv.at[0, d], s_recv.at[0, d])
-                    svec[1, d] = svec[0, d] + srecv[0, d, 0] + srecv[0, d, 1] + srecv[0, d, 2]
-                    begin(s_copies(1, d))
-            if st == 2 and s == 5:
-                tot = jnp.zeros((16, TILE), F32)
-                for d in range(3):
-                    arrive(srecv.at[1, d], s_recv.at[1, d])
-                    tot = tot + ((svec[1, d] + srecv[1, d, 0]) + (srecv[1, d, 1] + srecv[1, d, 2]))
-                stot[...] = tot
-                begin([sp_copy()])
-
         def unpack_wait(st):
             for k in range(COLORS):
                 arrive(kg.at[core, 0:BLK], dd_recv.at[st, k])
@@ -348,10 +350,8 @@
                         sup, m = UNITS[st][k // 2]
                         jrng = pl.ds((4 * m + 2 * c + k % 2) * TILE, TILE)
                         for a in range(4):
-                            src = kg[c, pl.ds(base(st, k) + a * TILE, TILE), :]
                             srng = pl.ds((4 * sup + a) * TILE, TILE)
-                            kfull[srng, jrng] = src
-                            kfull[jrng, srng] = src.T
+                            kfull[jrng, srng] = kfull[srng, jrng].T
                     continue
                 for sup in range(4):
                     for t, (i, j) in enumerate(OFFS[c]):
@@ -375,23 +375,19 @@
                 grad = -((th - mu_ref[...]) * lam_ref[...] + low)
                 adrv[rows, :] = (grad - rep_coef * th).astype(BF16)
 
-        def product(start, cols):
-            return jnp.dot(kfull[pl.ds(start, 256), cols[0]:cols[1]], adrv[cols[0]:cols[1], :], preferred_element_type=F32)
-
-        def update(chs, early=()):
+        def product(start):
+            return jnp.dot(kfull[pl.ds(start, 256), :], adrv[...], preferred_element_type=F32)
+
+        def update(chs, st):
             starts = [ch * BLK + half * 256 for ch in chs for half in range(2)]
             tot = stot[...] + spart[...] + 1.0
 
-            def whole(n):
-                if n < len(early):
-                    return early[n] + product(starts[n], (2 * BLK, ROWS))
-                return product(starts[n], (0, ROWS))
-
-            ahead = whole(0)
+            ahead = product(starts[0])
+            unpack(st)
             for n, start in enumerate(starts):
                 acc = ahead
                 if n + 1 < len(starts):
-                    ahead = whole(n + 1)
+                    ahead = product(starts[n + 1])
                 rows = pl.ds(start, 256)
                 sums = []
                 for blk in (start // TILE, start // TILE + 1):
@@ -407,7 +403,7 @@
                 th = jnp.concatenate(new, axis=1)
                 out_ref[rows, :] = th
                 prepare(start, 256, th)
-                if n % 2 == 1:
+                if n % 2 == 1 and chs[n // 2] < 3:
                     begin([pre_copy(chs[n // 2], 1), pre_copy(chs[n // 2], 0)])
 
         for s in range(5):
@@ -421,13 +417,10 @@
         advance(2, 5)
         remote(pack.at[0:5120], pack.at[0:5120], pre_send, sp_recv, mate).wait_send()
         unpack_wait(1)
-        unpack(1)
         arrive(stot, sp_recv)
-        update((0,))
+        update((0,), 1)
         unpack_wait(2)
-        early = [product(BLK + half * 256, (0, 2 * BLK)) for half in range(2)]
-        unpack(2)
-        update((1, 2, 3), early)
+        update((1, 2, 3), 2)
         for st in range(3):
             total = pack.at[0:SENT + (SENT_SUMS if st == 2 else 0)]
             remote(total, total, sent.at[st], sp_recv, mate).wait_send()
@@ -435,10 +428,10 @@
         return carry
 
     lax.fori_loop(0, NUM_STEPS, one_step, 0)
-    for ch in range(4):
+    for ch in range(3):
         for what in range(2):
             pre_copy(ch, what).wait_recv()
-    remote(pack.at[0:5120], pack.at[0:5120], pre_send, sp_recv, mate).wait_send()
+    remote(pack.at[0:3840], pack.at[0:3840], pre_send, sp_recv, mate).wait_send()
 
 
 def solution(mesh):
@@ -465,7 +458,7 @@
                     vm((3 * SROWS, TILE), F32),
                     vm((3, COLORS, BLK // 2, TILE), F32), vm((3, COLORS, BLK // 4, TILE), F32),
                     vm((3, COLORS, 3, OWN, TILE), F32), vm((3, COLORS, 4, OWN, TILE), F32),
-                    vm((2, 3 * SROWS, TILE), BF16), vm((ROWS, ROWS), BF16), vm((ROWS, loc), BF16),
+                    vm((2, SROWS, TILE), BF16), vm((ROWS, ROWS), BF16), vm((ROWS, loc), BF16),
                     vm((2, 3, 16, TILE), F32), vm((2, 3, 3, 16, TILE), F32), vm((16, TILE), F32), vm((16, TILE), F32),
                     dma((7,)), dma, dma((2, 4)), dma((3,)), dma((3, 2, COLORS)), dma((3, 3, COLORS)), dma((3, COLORS, 3)), dma((3, COLORS)),
                     dma((2, 3)), dma,

time: 155 us -> 152 us (0.981)
  Pallas kernels: 153 us -> 150 us
    pallas_call x1, Pallas kernels: 153 us -> 150 us  [local_steps(): call(hbm(current), hbm(prec_loc.reshape(1, loc)), hbm(mean_loc.reshape(1,...]
where the time goes in v6:
time: 152 us
  Pallas kernels  150 us (99%)
  local copies, waits for them, and re-layouts  2.02 us (1%)
    pallas_call x1, Pallas kernels, local_steps(): call(hbm(current), hbm(prec_loc.reshape(1, loc)), hbm(mean_loc.reshape(1,...  150 us

profile of v6, /device:TPU:1, one launch (start us, length us, event | category | flops | bytes accessed | tf_op | source)
XLA Modules:
  0.0 151.5 jit_solution(1570923558182393757)
XLA Ops:
  0.0 149.5 %svgd.1 = f32[2048,512]{1,0:T(8,128)S(1)} custom-call(f32[2048,512]{1,0:T(8,128)} %theta_ref.1, f32[1,512]{1,0:T(1,128)} %bitcast.2, f32[1,512]{1,0:T(1,128)} %bitcast.3, bf16[512,128]{1,0:T(8,128)(2,1)} %fac_hbm.1), custom_call_target="tpu_custom_call" | custom-call | tf_op jit(solution)/shard_map/svgd/pallas_call | solution.py:470
  149.5 2.0 %copy.6 = f32[2048,512]{1,0:T(8,128)} copy(f32[2048,512]{1,0:T(8,128)S(1)} %svgd.1) | data formatting | bytes 8388608

commit v7 on v6

--- a/solution.py
+++ b/solution.py
@@ -127,13 +127,13 @@
     def remote(src, dst, ssem, rsem, where):
         return pltpu.make_async_remote_copy(src_ref=src, dst_ref=dst, send_sem=ssem, recv_sem=rsem, device_id=where, device_id_type=MESH)
 
-    def pre_copy(ch, what):
-        if what == 0:
-            rows = pl.ds(ch * BLK, BLK)
-            src, dst = bfull.at[rows, 0:width], bfull.at[rows, width:2 * width]
-        else:
-            src, dst = pml.at[pl.ds(al(ch * BLK + (1 - core) * 256), 256)], pmr.at[pl.ds(ch * 256, 256)]
-        return remote(src, dst, pre_send, pre_recv.at[what, ch], mate)
+    def pre_bf16(piece):
+        rows = pl.ds(piece * 256, 256)
+        return remote(bfull.at[rows, 0:width], bfull.at[rows, width:2 * width], pre_send, pre_recv.at[piece], mate)
+
+    def pre_pm(ch):
+        src, dst = pml.at[pl.ds(al(ch * BLK + (1 - core) * 256), 256)], pmr.at[pl.ds(ch * 256, 256)]
+        return remote(src, dst, pre_send, pre_recv.at[8 + ch], mate)
 
     def prepare(start, length, th):
         rows = pl.ds(start, length)
@@ -235,32 +235,41 @@
 
     def pm_tiles(half):
         for ch in (2 * half, 2 * half + 1):
-            pre_copy(ch, 1).wait_recv()
+            pre_pm(ch).wait_recv()
             mine = pl.ds(al(ch * BLK + core * 256), 256)
             pack[pl.ds(PM_ROW + ch * 256, 256), :] = pml[mine, :] + pmr[pl.ds(ch * 256, 256), :]
         begin([rs_copy(0, 0, 4 + half)])
 
     def open_step():
-        begin([pre_copy(3, 1), pre_copy(3, 0)])
-        for half in range(2):
-            pm_tiles(half)
-            gs = []
-            for m in (2 * half, 2 * half + 1):
-                pre_copy(m, 0).wait_recv()
-            for m in (2 * half, 2 * half + 1):
-                gs.append(products(m))
-                norms(m)
-            for n in range(2):
-                tiles(2 * half + n, gs[n])
+        begin([pre_pm(3), pre_bf16(7)])
+        pm_tiles(0)
+        for piece in range(4):
+            pre_bf16(piece).wait_recv()
+        gs = []
+        for m in range(2):
+            gs.append(products(m))
+            norms(m)
+        for m in range(2):
+            tiles(m, gs[m])
+        for m in range(2, 4):
+            for piece in range(2 * m, 2 * m + 2):
+                pre_bf16(piece).wait_recv()
+            g = products(m)
+            norms(m)
+            tiles(m, g)
+            if m == 2:
+                pm_tiles(1)
 
     for cp in loads[4:]:
         cp.wait()
     for ch in range(4):
         loads[ch].wait()
         prepare(ch * BLK, BLK, out_ref[pl.ds(ch * BLK, BLK), :])
-    pl.semaphore_wait(barrier, 10)
-    for ch in range(3):
-        begin([pre_copy(ch, 1), pre_copy(ch, 0)])
+        if ch == 0:
+            pl.semaphore_wait(barrier, 10)
+        if ch < 3:
+            begin([pre_pm(ch)])
+        begin([pre_bf16(piece) for piece in (2 * ch, 2 * ch + 1) if piece < 7])
     open_step()
 
     def one_step(step_index, carry):
@@ -378,33 +387,27 @@
         def product(start):
             return jnp.dot(kfull[pl.ds(start, 256), :], adrv[...], preferred_element_type=F32)
 
-        def update(chs, st):
-            starts = [ch * BLK + half * 256 for ch in chs for half in range(2)]
-            tot = stot[...] + spart[...] + 1.0
-
-            ahead = product(starts[0])
-            unpack(st)
-            for n, start in enumerate(starts):
-                acc = ahead
-                if n + 1 < len(starts):
-                    ahead = product(starts[n + 1])
-                rows = pl.ds(start, 256)
-                sums = []
-                for blk in (start // TILE, start // TILE + 1):
-                    line = jnp.where(eye, jnp.broadcast_to(tot[blk:blk + 1, :], (TILE, TILE)), 0.0)
-                    sums.append(rep_coef * jnp.sum(line, axis=1, keepdims=True))
-                sums = jnp.broadcast_to(jnp.concatenate(sums, axis=0), (256, TILE))
-                new = []
-                for t in range(width // TILE):
-                    cols = slice(t * TILE, (t + 1) * TILE)
-                    th = out_ref[rows, cols]
-                    phi = (acc[:, cols] + sums * th) / n_part
-                    new.append(th + step_size * phi)
-                th = jnp.concatenate(new, axis=1)
-                out_ref[rows, :] = th
-                prepare(start, 256, th)
-                if n % 2 == 1 and chs[n // 2] < 3:
-                    begin([pre_copy(chs[n // 2], 1), pre_copy(chs[n // 2], 0)])
+        def finish(start, acc, tot):
+            rows = pl.ds(start, 256)
+            sums = []
+            for blk in (start // TILE, start // TILE + 1):
+                line = jnp.where(eye, jnp.broadcast_to(tot[blk:blk + 1, :], (TILE, TILE)), 0.0)
+                sums.append(rep_coef * jnp.sum(line, axis=1, keepdims=True))
+            sums = jnp.broadcast_to(jnp.concatenate(sums, axis=0), (256, TILE))
+            new = []
+            for t in range(width // TILE):
+                cols = slice(t * TILE, (t + 1) * TILE)
+                th = out_ref[rows, cols]
+                phi = (acc[:, cols] + sums * th) / n_part
+                new.append(th + step_size * phi)
+            th = jnp.concatenate(new, axis=1)
+            out_ref[rows, :] = th
+            prepare(start, 256, th)
+            piece = start // 256
+            if piece == 6:
+                begin([pre_bf16(6)])
+            elif piece in (1, 3, 5):
+                begin([pre_pm(piece // 2), pre_bf16(piece - 1), pre_bf16(piece)])
 
         for s in range(5):
             for st in range(3):
@@ -416,11 +419,21 @@
         drive()
         advance(2, 5)
         remote(pack.at[0:5120], pack.at[0:5120], pre_send, sp_recv, mate).wait_send()
+        def update(starts, st):
+            tot = stot[...] + spart[...] + 1.0
+            ahead = product(starts[0])
+            unpack(st)
+            for n, start in enumerate(starts):
+                acc = ahead
+                if n + 1 < len(starts):
+                    ahead = product(starts[n + 1])
+                finish(start, acc, tot)
+
         unpack_wait(1)
         arrive(stot, sp_recv)
-        update((0,), 1)
+        update(range(0, BLK, 256), 1)
         unpack_wait(2)
-        update((1, 2, 3), 2)
+        update(range(BLK, ROWS, 256), 2)
         for st in range(3):
             total = pack.at[0:SENT + (SENT_SUMS if st == 2 else 0)]
             remote(total, total, sent.at[st], sp_recv, mate).wait_send()
@@ -429,9 +442,11 @@
 
     lax.fori_loop(0, NUM_STEPS, one_step, 0)
     for ch in range(3):
-        for what in range(2):
-            pre_copy(ch, what).wait_recv()
-    remote(pack.at[0:3840], pack.at[0:3840], pre_send, sp_recv, mate).wait_send()
+        pre_pm(ch).wait_recv()
+    for piece in range(7):
+        pre_bf16(piece).wait_recv()
+    total = pack.at[0:7 * 512 + 3 * 256]
+    remote(total, total, pre_send, sp_recv, mate).wait_send()
 
 
 def solution(mesh):
@@ -460,7 +475,7 @@
                     vm((3, COLORS, 3, OWN, TILE), F32), vm((3, COLORS, 4, OWN, TILE), F32),
                     vm((2, SROWS, TILE), BF16), vm((ROWS, ROWS), BF16), vm((ROWS, loc), BF16),
                     vm((2, 3, 16, TILE), F32), vm((2, 3, 3, 16, TILE), F32), vm((16, TILE), F32), vm((16, TILE), F32),
-                    dma((7,)), dma, dma((2, 4)), dma((3,)), dma((3, 2, COLORS)), dma((3, 3, COLORS)), dma((3, COLORS, 3)), dma((3, COLORS)),
+                    dma((7,)), dma, dma((12,)), dma((3,)), dma((3, 2, COLORS)), dma((3, 3, COLORS)), dma((3, COLORS, 3)), dma((3, COLORS)),
                     dma((2, 3)), dma,
                 ],
                 compiler_params=pltpu.CompilerParams(collective_id=0, has_side_effects=True, vmem_limit_bytes=50000000),

time: 152 us -> 154 us (1.013)
  Pallas kernels: 150 us -> 152 us
    pallas_call x1, Pallas kernels: 150 us -> 152 us  [local_steps(): call(hbm(current), hbm(prec_loc.reshape(1, loc)), hbm(mean_loc.reshape(1,...]
where the time goes in v7:
time: 154 us
  Pallas kernels  152 us (99%)
  local copies, waits for them, and re-layouts  2.02 us (1%)
    pallas_call x1, Pallas kernels, local_steps(): call(hbm(current), hbm(prec_loc.reshape(1, loc)), hbm(mean_loc.reshape(1,...  152 us

profile of v7, /device:TPU:1, one launch (start us, length us, event | category | flops | bytes accessed | tf_op | source)
XLA Modules:
  0.0 154.1 jit_solution(5805184561807291003)
XLA Ops:
  0.0 152.1 %svgd.1 = f32[2048,512]{1,0:T(8,128)S(1)} custom-call(f32[2048,512]{1,0:T(8,128)} %theta_ref.1, f32[1,512]{1,0:T(1,128)} %bitcast.2, f32[1,512]{1,0:T(1,128)} %bitcast.3, bf16[512,128]{1,0:T(8,128)(2,1)} %fac_hbm.1), custom_call_target="tpu_custom_call" | custom-call | tf_op jit(solution)/shard_map/svgd/pallas_call | solution.py:485
  152.1 2.0 %copy.6 = f32[2048,512]{1,0:T(8,128)} copy(f32[2048,512]{1,0:T(8,128)S(1)} %svgd.1) | data formatting | bytes 8388608

commit v8 on v7

--- a/solution.py
+++ b/solution.py
@@ -21,7 +21,7 @@
 UNITS = ((), ((0, 3), (0, 1), (0, 2)), ((1, 2), (1, 3), (2, 3)))
 OFFS = (((0, 1), (2, 0), (3, 0)), ((1, 2), (1, 3), (2, 3)))
 PM_ROW = 4 * BLK
-SENT = 1536 + 768 + 576 + 576 + 288 + 1152 + 1536
+SENT = 1536 + 768 + 576 + 576 + 576 + 864 + 1536
 SENT_SUMS = 288 + 16
 OWN = 32
 MESH = pl.DeviceIdType.MESH
@@ -42,7 +42,7 @@
     theta_ref, lam_hbm, mu_hbm, fac_hbm, out_ref,
     lam_ref, mu_ref, fac_ref,
     bfull, pml, pmr, nrow, ncol, pack, r0, r1, r2, r3, kg, kfull, adrv, svec, srecv, stot, spart,
-    in_sem, pre_send, pre_recv, sent, rs_recv, x_recv, far_recv, dd_recv, s_recv, sp_recv,
+    in_sem, pre_send, pre_recv, sent, rs_recv, x_recv, near_recv, far_recv, dd_recv, s_recv, sp_recv,
 ):
     width = out_ref.shape[1]
     rep_coef = 2.0 / bandwidth
@@ -148,7 +148,7 @@
         remote(ref, ref, sent.at[0], sem, mate).wait_recv()
 
     def x_arrive(st, e, k):
-        arrive((r2.at[st, k], r3.at[st, k, 0:3], kg.at[core, 0:3 * OWN])[e], x_recv.at[st, e, k])
+        arrive((r2.at[st, k], r3.at[st, k, 0:3])[e], x_recv.at[st, e, k])
 
     def rs_copy(st, s, k):
         peer, length, keep, give = halves[k][s]
@@ -163,19 +163,23 @@
 
     def x_copies(st, e, k):
         d1, d2, d3 = dims(k)
-        dim = (d2, d3, d2, d1)[e]
+        dim = (d2, d3)[e]
         cps = []
         for j in range(1, 4):
             if e == 0:
                 src = pack.at[pl.ds(al(quarter(st, k) + pieces[k][j]), OWN)]
                 dst = r2.at[st, k, j - 1]
-            elif e == 1:
+            else:
                 src = dst = r3.at[st, k, coords[dim]]
-            else:
-                start = (own if e == 2 else quarter)(0, k) - base(0, k)
-                src = dst = gathered(st, k, start, OWN if e == 2 else TILE)
-            arrived = far_recv.at[st, k, j - 1] if e == 3 else x_recv.at[st, e, k]
-            cps.append(remote(src, dst, sent.at[st], arrived, ring[dim][j]))
+            cps.append(remote(src, dst, sent.at[st], x_recv.at[st, e, k], ring[dim][j]))
+        return cps
+
+    def gather_copies(st, k, j):
+        d1, d2, d3 = dims(k)
+        ref = gathered(st, k, halves[k][1][2] + pieces[k][(4 - j) % 4], OWN)
+        cps = [remote(ref, ref, sent.at[st], far_recv.at[st, k, i - 1], ring[d1][i]) for i in range(1, 4)]
+        if j == 0:
+            cps = [remote(ref, ref, sent.at[st], near_recv.at[st, k, i - 1], ring[d2][i]) for i in range(1, 4)] + cps
         return cps
 
     def dd_copy(st, k, j):
@@ -251,14 +255,13 @@
             norms(m)
         for m in range(2):
             tiles(m, gs[m])
+        pm_tiles(1)
         for m in range(2, 4):
             for piece in range(2 * m, 2 * m + 2):
                 pre_bf16(piece).wait_recv()
             g = products(m)
             norms(m)
             tiles(m, g)
-            if m == 2:
-                pm_tiles(1)
 
     for cp in loads[4:]:
         cp.wait()
@@ -331,15 +334,16 @@
                         kern = jnp.exp(-jnp.maximum(full, 0.0) / bandwidth)
                         parts[k % 3] += row_sums(st, k, kern)
                     gathered(st, k, own(0, k) - base(0, k), OWN)[...] = kern.astype(BF16)
-                    begin(x_copies(st, 2, k))
+                    begin(gather_copies(st, k, 0))
                 elif s == 4:
-                    x_arrive(st, 2, k)
-                    begin(x_copies(st, 3, k))
+                    for j in range(1, 4):
+                        arrive(kg.at[core, 0:OWN], near_recv.at[st, k, j - 1])
+                        begin(gather_copies(st, k, j))
                     begin([dd_copy(st, k, 0)])
                 else:
-                    for j, cp in enumerate(x_copies(st, 3, k)):
-                        cp.wait_recv()
-                        begin([dd_copy(st, k, j + 1)])
+                    for j in range(1, 4):
+                        arrive(kg.at[core, 0:TILE], far_recv.at[st, k, j - 1])
+                        begin([dd_copy(st, k, j)])
             if s == 3:
                 for d in range(3):
                     if st == 0:
@@ -475,7 +479,7 @@
                     vm((3, COLORS, 3, OWN, TILE), F32), vm((3, COLORS, 4, OWN, TILE), F32),
                     vm((2, SROWS, TILE), BF16), vm((ROWS, ROWS), BF16), vm((ROWS, loc), BF16),
                     vm((2, 3, 16, TILE), F32), vm((2, 3, 3, 16, TILE), F32), vm((16, TILE), F32), vm((16, TILE), F32),
-                    dma((7,)), dma, dma((12,)), dma((3,)), dma((3, 2, COLORS)), dma((3, 3, COLORS)), dma((3, COLORS, 3)), dma((3, COLORS)),
+                    dma((7,)), dma, dma((12,)), dma((3,)), dma((3, 2, COLORS)), dma((3, 2, COLORS)), dma((3, COLORS, 3)), dma((3, COLORS, 3)), dma((3, COLORS)),
                     dma((2, 3)), dma,
                 ],
                 compiler_params=pltpu.CompilerParams(collective_id=0, has_side_effects=True, vmem_limit_bytes=50000000),

time: 154 us -> 150 us (0.974)
  Pallas kernels: 152 us -> 148 us
    pallas_call x1, Pallas kernels: 152 us -> 148 us  [local_steps(): call(hbm(current), hbm(prec_loc.reshape(1, loc)), hbm(mean_loc.reshape(1,...]
where the time goes in v8:
time: 150 us
  Pallas kernels  148 us (99%)
  local copies, waits for them, and re-layouts  2.02 us (1%)
    pallas_call x1, Pallas kernels, local_steps(): call(hbm(current), hbm(prec_loc.reshape(1, loc)), hbm(mean_loc.reshape(1,...  148 us

profile of v8, /device:TPU:1, one launch (start us, length us, event | category | flops | bytes accessed | tf_op | source)
XLA Modules:
  0.0 149.8 jit_solution(17450761282861234363)
XLA Ops:
  0.0 147.8 %svgd.1 = f32[2048,512]{1,0:T(8,128)S(1)} custom-call(f32[2048,512]{1,0:T(8,128)} %theta_ref.1, f32[1,512]{1,0:T(1,128)} %bitcast.2, f32[1,512]{1,0:T(1,128)} %bitcast.3, bf16[512,128]{1,0:T(8,128)(2,1)} %fac_hbm.1), custom_call_target="tpu_custom_call" | custom-call | tf_op jit(solution)/shard_map/svgd/pallas_call | solution.py:489
  147.8 2.0 %copy.6 = f32[2048,512]{1,0:T(8,128)} copy(f32[2048,512]{1,0:T(8,128)S(1)} %svgd.1) | data formatting | bytes 8388608

commit v9 on v8

--- a/solution.py
+++ b/solution.py
@@ -15,15 +15,17 @@
 
 ROWS = 2048
 TILE = 128
-BLK = 512
+HALF = 256
+BLK = 2 * HALF
 COLORS = 6
 SROWS = COLORS * BLK
 UNITS = ((), ((0, 3), (0, 1), (0, 2)), ((1, 2), (1, 3), (2, 3)))
 OFFS = (((0, 1), (2, 0), (3, 0)), ((1, 2), (1, 3), (2, 3)))
 PM_ROW = 4 * BLK
-SENT = 1536 + 768 + 576 + 576 + 576 + 864 + 1536
-SENT_SUMS = 288 + 16
+SENT = 6432
+SENT_SUMS = 304
 OWN = 32
+PEERS = range(1, 4)
 MESH = pl.DeviceIdType.MESH
 NT = (((1,), (1,)), ((), ()))
 F32, BF16 = jnp.float32, jnp.bfloat16
@@ -41,7 +43,7 @@
     bandwidth, step_size, n_part,
     theta_ref, lam_hbm, mu_hbm, fac_hbm, out_ref,
     lam_ref, mu_ref, fac_ref,
-    bfull, pml, pmr, nrow, ncol, pack, r0, r1, r2, r3, kg, kfull, adrv, svec, srecv, stot, spart,
+    bfull, pml, pmr, nrow, ncol, pulled, scaled, pack, r0, r1, r2, r3, kg, kfull, adrv, svec, srecv, stot, spart,
     in_sem, pre_send, pre_recv, sent, rs_recv, x_recv, near_recv, far_recv, dd_recv, s_recv, sp_recv,
 ):
     width = out_ref.shape[1]
@@ -54,7 +56,7 @@
     def chip(dim, coord):
         return {"feat": feat + (coord - coords[dim]) * strides[dim]}
 
-    turned = [[coords[dim]] + [rem(coords[dim] + j, 4) for j in range(1, 4)] for dim in range(3)]
+    turned = [[coords[dim]] + [rem(coords[dim] + j, 4) for j in PEERS] for dim in range(3)]
 
     def around(dim, j):
         return turned[dim][j]
@@ -108,7 +110,7 @@
     barrier = pltpu.get_barrier_semaphore()
     pl.semaphore_signal(barrier, inc=1, device_id=mate, device_id_type=MESH)
     for dim in range(3):
-        for j in range(1, 4):
+        for j in PEERS:
             pl.semaphore_signal(barrier, inc=1, device_id=ring[dim][j], device_id_type=MESH)
     loads = [pltpu.make_async_copy(theta_ref.at[pl.ds(ch * BLK, BLK)], out_ref.at[pl.ds(ch * BLK, BLK)], in_sem.at[ch]) for ch in range(4)]
     loads += [
@@ -128,17 +130,20 @@
         return pltpu.make_async_remote_copy(src_ref=src, dst_ref=dst, send_sem=ssem, recv_sem=rsem, device_id=where, device_id_type=MESH)
 
     def pre_bf16(piece):
-        rows = pl.ds(piece * 256, 256)
+        rows = pl.ds(piece * HALF, HALF)
         return remote(bfull.at[rows, 0:width], bfull.at[rows, width:2 * width], pre_send, pre_recv.at[piece], mate)
 
     def pre_pm(ch):
-        src, dst = pml.at[pl.ds(al(ch * BLK + (1 - core) * 256), 256)], pmr.at[pl.ds(ch * 256, 256)]
+        src, dst = pml.at[pl.ds(al(ch * BLK + (1 - core) * HALF), HALF)], pmr.at[pl.ds(ch * HALF, HALF)]
         return remote(src, dst, pre_send, pre_recv.at[8 + ch], mate)
 
-    def prepare(start, length, th):
-        rows = pl.ds(start, length)
-        bfull[rows, 0:width] = th.astype(BF16)
-        pml[rows, :] = jnp.dot((th - mu_ref[...]).astype(BF16), fac_ref[...], preferred_element_type=F32)
+    def prepare(start, th):
+        bfull[pl.ds(start, HALF), 0:width] = th.astype(BF16)
+        return (th - mu_ref[...]).astype(BF16)
+
+    def partial_pm(start, centered):
+        for n, rows in enumerate(centered):
+            pml[pl.ds(start + HALF * n, HALF), :] = jnp.dot(rows, fac_ref[...], preferred_element_type=F32)
 
     def begin(cps):
         for cp in cps:
@@ -165,7 +170,7 @@
         d1, d2, d3 = dims(k)
         dim = (d2, d3)[e]
         cps = []
-        for j in range(1, 4):
+        for j in PEERS:
             if e == 0:
                 src = pack.at[pl.ds(al(quarter(st, k) + pieces[k][j]), OWN)]
                 dst = r2.at[st, k, j - 1]
@@ -177,9 +182,9 @@
     def gather_copies(st, k, j):
         d1, d2, d3 = dims(k)
         ref = gathered(st, k, halves[k][1][2] + pieces[k][(4 - j) % 4], OWN)
-        cps = [remote(ref, ref, sent.at[st], far_recv.at[st, k, i - 1], ring[d1][i]) for i in range(1, 4)]
+        cps = [remote(ref, ref, sent.at[st], far_recv.at[st, k, i - 1], ring[d1][i]) for i in PEERS]
         if j == 0:
-            cps = [remote(ref, ref, sent.at[st], near_recv.at[st, k, i - 1], ring[d2][i]) for i in range(1, 4)] + cps
+            cps = [remote(ref, ref, sent.at[st], near_recv.at[st, k, i - 1], ring[d2][i]) for i in PEERS] + cps
         return cps
 
     def dd_copy(st, k, j):
@@ -190,15 +195,15 @@
         dim = ((d + 1) % 3, d)[ph]
         return [
             remote(svec.at[ph, d], srecv.at[ph, d, j - 1], sent.at[2], s_recv.at[ph, d], ring[dim][j])
-            for j in range(1, 4)
+            for j in PEERS
         ]
 
     def sp_copy():
         return remote(stot, spart, sent.at[2], sp_recv, mate)
 
     def products(m):
-        mine = bfull[pl.ds(al(m * BLK + 256 * core), 256), :]
-        part = BLK if m == 3 else (m + 1) * 256
+        mine = bfull[pl.ds(al(m * BLK + HALF * core), HALF), :]
+        part = BLK if m == 3 else (m + 1) * HALF
         return [lax.dot_general(bfull[pl.ds(at, part), :], mine, NT, preferred_element_type=F32) for at in range(0, (m + 1) * BLK, part)]
 
     def norms(m):
@@ -211,7 +216,7 @@
 
     def tiles(m, g):
         def block(blk, b):
-            n, r = divmod(blk * TILE, BLK if m == 3 else (m + 1) * 256)
+            n, r = divmod(blk * TILE, BLK if m == 3 else (m + 1) * HALF)
             return g[n][r:r + TILE, b * TILE:(b + 1) * TILE]
 
         def tile(i, b):
@@ -240,8 +245,8 @@
     def pm_tiles(half):
         for ch in (2 * half, 2 * half + 1):
             pre_pm(ch).wait_recv()
-            mine = pl.ds(al(ch * BLK + core * 256), 256)
-            pack[pl.ds(PM_ROW + ch * 256, 256), :] = pml[mine, :] + pmr[pl.ds(ch * 256, 256), :]
+            mine = pl.ds(al(ch * BLK + core * HALF), HALF)
+            pack[pl.ds(PM_ROW + ch * HALF, HALF), :] = pml[mine, :] + pmr[pl.ds(ch * HALF, HALF), :]
         begin([rs_copy(0, 0, 4 + half)])
 
     def open_step():
@@ -267,7 +272,8 @@
         cp.wait()
     for ch in range(4):
         loads[ch].wait()
-        prepare(ch * BLK, BLK, out_ref[pl.ds(ch * BLK, BLK), :])
+        starts = (ch * BLK, ch * BLK + HALF)
+        partial_pm(ch * BLK, [prepare(start, out_ref[pl.ds(start, HALF), :]) for start in starts])
         if ch == 0:
             pl.semaphore_wait(barrier, 10)
         if ch < 3:
@@ -336,12 +342,12 @@
                     gathered(st, k, own(0, k) - base(0, k), OWN)[...] = kern.astype(BF16)
                     begin(gather_copies(st, k, 0))
                 elif s == 4:
-                    for j in range(1, 4):
+                    for j in PEERS:
                         arrive(kg.at[core, 0:OWN], near_recv.at[st, k, j - 1])
                         begin(gather_copies(st, k, j))
                     begin([dd_copy(st, k, 0)])
                 else:
-                    for j in range(1, 4):
+                    for j in PEERS:
                         arrive(kg.at[core, 0:TILE], far_recv.at[st, k, j - 1])
                         begin([dd_copy(st, k, j)])
             if s == 3:
@@ -379,40 +385,49 @@
                     kfull[ra, ra] = jnp.where(upper, src, jnp.where(lower, srt, one))
                     kfull[rb, rb] = jnp.where(lower, src, jnp.where(upper, srt, one))
 
+        def drive_parts():
+            for q in range(8):
+                rows = pl.ds(q * HALF, HALF)
+                th = out_ref[rows, :]
+                pulled[rows, :] = (th - mu_ref[...]) * lam_ref[...]
+                scaled[rows, :] = rep_coef * th
+
         def drive():
             for q in range(8):
-                rows = pl.ds(q * 256, 256)
-                pm = kg[q % 2, pl.ds(PM_ROW + (q // 2) * 256, 256), :]
+                rows = pl.ds(q * HALF, HALF)
+                pm = kg[q % 2, pl.ds(PM_ROW + (q // 2) * HALF, HALF), :]
                 low = lax.dot_general(pm, fac_ref[...], NT, preferred_element_type=F32)
-                th = out_ref[rows, :]
-                grad = -((th - mu_ref[...]) * lam_ref[...] + low)
-                adrv[rows, :] = (grad - rep_coef * th).astype(BF16)
+                adrv[rows, :] = ((pulled[rows, :] + low) + scaled[rows, :]).astype(BF16)
 
         def product(start):
-            return jnp.dot(kfull[pl.ds(start, 256), :], adrv[...], preferred_element_type=F32)
-
-        def finish(start, acc, tot):
-            rows = pl.ds(start, 256)
+            return jnp.dot(kfull[pl.ds(start, HALF), :], adrv[...], preferred_element_type=F32)
+
+        def finish(start, acc, tot, held):
+            rows = pl.ds(start, HALF)
             sums = []
             for blk in (start // TILE, start // TILE + 1):
                 line = jnp.where(eye, jnp.broadcast_to(tot[blk:blk + 1, :], (TILE, TILE)), 0.0)
                 sums.append(rep_coef * jnp.sum(line, axis=1, keepdims=True))
-            sums = jnp.broadcast_to(jnp.concatenate(sums, axis=0), (256, TILE))
+            sums = jnp.broadcast_to(jnp.concatenate(sums, axis=0), (HALF, TILE))
             new = []
             for t in range(width // TILE):
                 cols = slice(t * TILE, (t + 1) * TILE)
                 th = out_ref[rows, cols]
-                phi = (acc[:, cols] + sums * th) / n_part
+                phi = (sums * th - acc[:, cols]) / n_part
                 new.append(th + step_size * phi)
             th = jnp.concatenate(new, axis=1)
             out_ref[rows, :] = th
-            prepare(start, 256, th)
-            piece = start // 256
-            if piece == 6:
-                begin([pre_bf16(6)])
-            elif piece in (1, 3, 5):
-                begin([pre_pm(piece // 2), pre_bf16(piece - 1), pre_bf16(piece)])
-
+            held.append(prepare(start, th))
+            if start % BLK:
+                partial_pm(start - HALF, held[-2:])
+
+        def share(start):
+            if start % BLK and start + HALF < ROWS:
+                begin([pre_pm(start // BLK), pre_bf16(start // HALF - 1), pre_bf16(start // HALF)])
+            elif start + BLK == ROWS:
+                begin([pre_bf16(start // HALF)])
+
+        drive_parts()
         for s in range(5):
             for st in range(3):
                 advance(st, s)
@@ -427,17 +442,21 @@
             tot = stot[...] + spart[...] + 1.0
             ahead = product(starts[0])
             unpack(st)
+            held = []
             for n, start in enumerate(starts):
                 acc = ahead
                 if n + 1 < len(starts):
                     ahead = product(starts[n + 1])
-                finish(start, acc, tot)
+                if n:
+                    share(starts[n - 1])
+                finish(start, acc, tot, held)
+            share(starts[-1])
 
         unpack_wait(1)
         arrive(stot, sp_recv)
-        update(range(0, BLK, 256), 1)
+        update(range(0, BLK, HALF), 1)
         unpack_wait(2)
-        update(range(BLK, ROWS, 256), 2)
+        update(range(BLK, ROWS, HALF), 2)
         for st in range(3):
             total = pack.at[0:SENT + (SENT_SUMS if st == 2 else 0)]
             remote(total, total, sent.at[st], sp_recv, mate).wait_send()
@@ -449,7 +468,7 @@
         pre_pm(ch).wait_recv()
     for piece in range(7):
         pre_bf16(piece).wait_recv()
-    total = pack.at[0:7 * 512 + 3 * 256]
+    total = pack.at[0:7 * 512 + 3 * HALF]
     remote(total, total, pre_send, sp_recv, mate).wait_send()
 
 
@@ -473,7 +492,7 @@
                 scratch_shapes=[
                     vm((1, loc), F32), vm((1, loc), F32), vm((loc, rank), BF16),
                     vm((ROWS, 2 * loc), BF16), vm((ROWS, rank), F32), vm((ROWS // 2, rank), F32),
-                    vm((ROWS, TILE), F32), vm((16, TILE), F32),
+                    vm((ROWS, TILE), F32), vm((16, TILE), F32), vm((ROWS, loc), F32), vm((ROWS, loc), F32),
                     vm((3 * SROWS, TILE), F32),
                     vm((3, COLORS, BLK // 2, TILE), F32), vm((3, COLORS, BLK // 4, TILE), F32),
                     vm((3, COLORS, 3, OWN, TILE), F32), vm((3, COLORS, 4, OWN, TILE), F32),

time: 150 us -> 149 us (level)
  no operation moved by 1% of the time
where the time goes in v9:
time: 149 us
  Pallas kernels  147 us (99%)
  local copies, waits for them, and re-layouts  2.02 us (1%)
    pallas_call x1, Pallas kernels, local_steps(): call(hbm(current), hbm(prec_loc.reshape(1, loc)), hbm(mean_loc.reshape(1,...  147 us

profile of v9, /device:TPU:1, one launch (start us, length us, event | category | flops | bytes accessed | tf_op | source)
XLA Modules:
  0.0 148.8 jit_solution(10571215530285947437)
XLA Ops:
  0.0 146.8 %svgd.1 = f32[2048,512]{1,0:T(8,128)S(1)} custom-call(f32[2048,512]{1,0:T(8,128)} %theta_ref.1, f32[1,512]{1,0:T(1,128)} %bitcast.2, f32[1,512]{1,0:T(1,128)} %bitcast.3, bf16[512,128]{1,0:T(8,128)(2,1)} %fac_hbm.1), custom_call_target="tpu_custom_call" | custom-call | tf_op jit(solution)/shard_map/svgd/pallas_call | solution.py:508
  146.8 2.0 %copy.6 = f32[2048,512]{1,0:T(8,128)} copy(f32[2048,512]{1,0:T(8,128)S(1)} %svgd.1) | data formatting | bytes 8388608

commit v10 on v9

--- a/solution.py
+++ b/solution.py
@@ -19,13 +19,15 @@
 BLK = 2 * HALF
 COLORS = 6
 SROWS = COLORS * BLK
+STREAMS = 6
+QUARTER = HALF // 4
 UNITS = ((), ((0, 3), (0, 1), (0, 2)), ((1, 2), (1, 3), (2, 3)))
 OFFS = (((0, 1), (2, 0), (3, 0)), ((1, 2), (1, 3), (2, 3)))
-PM_ROW = 4 * BLK
-SENT = 6432
+SENT = 3216
 SENT_SUMS = 304
-OWN = 32
-PEERS = range(1, 4)
+OWN = QUARTER // 4
+PEERS = (2, 1, 3)
+NEAR_FIRST = (1, 3, 2)
 MESH = pl.DeviceIdType.MESH
 NT = (((1,), (1,)), ((), ()))
 F32, BF16 = jnp.float32, jnp.bfloat16
@@ -56,7 +58,7 @@
     def chip(dim, coord):
         return {"feat": feat + (coord - coords[dim]) * strides[dim]}
 
-    turned = [[coords[dim]] + [rem(coords[dim] + j, 4) for j in PEERS] for dim in range(3)]
+    turned = [[coords[dim]] + [rem(coords[dim] + j, 4) for j in sorted(PEERS)] for dim in range(3)]
 
     def around(dim, j):
         return turned[dim][j]
@@ -74,7 +76,7 @@
     halves = []
     for k in range(COLORS):
         steps = []
-        start, length, cur = 0, BLK, coords[k % 3]
+        start, length, cur = 0, HALF, coords[k % 3]
         for s in range(2):
             if (k // 3 + s) % 2 == 0:
                 other, bit = cur + 1 - 2 * low_bit[k % 3], pair_bit[k % 3][0]
@@ -90,22 +92,23 @@
         return k % 3, (k + 1) % 3, (k + 2) % 3
 
     def base(st, k):
-        return st * SROWS + k * BLK
-
-    quarters = [[base(st, k) + halves[k][1][2] for k in range(COLORS)] for st in range(3)]
-    owns = [[quarters[st][k] + OWN * coords[dims(k)[1]] for k in range(COLORS)] for st in range(3)]
-    pieces = [[OWN * around(dims(k)[1], j) for j in range(4)] for k in range(COLORS)]
-
+        return (st * COLORS + k) * HALF
+
+    def tile_row(kind, k, a):
+        return base(2 * kind + a // 2, k) + a % 2 * TILE
+
+    keeps = [[al(step[2]) for step in steps] for steps in halves]
+    gives = [[al(step[3]) for step in steps] for steps in halves]
+    pieces = [[al(halves[k][1][2] + OWN * around(dims(k)[1], j)) for j in range(4)] for k in range(COLORS)]
     places = []
     for k in range(COLORS):
         one, two = (pair_bit, high_bit) if k < 3 else (high_bit, pair_bit)
-        places.append([TILE * (2 * one[k % 3][j] + two[k % 3][j]) for j in range(4)])
-
-    def quarter(st, k):
-        return quarters[st][k]
-
-    def own(st, k):
-        return owns[st][k]
+        places.append([al(QUARTER * (2 * one[k % 3][j] + two[k % 3][j])) for j in range(4)])
+
+    columns = [[al(m * BLK + (2 * core + n) * TILE, TILE) for n in range(2)] for m in range(4)]
+
+    def packed(st, k, row, rows):
+        return pack.at[pl.ds(al(base(st, k) + row), rows)]
 
     barrier = pltpu.get_barrier_semaphore()
     pl.semaphore_signal(barrier, inc=1, device_id=mate, device_id_type=MESH)
@@ -157,14 +160,14 @@
 
     def rs_copy(st, s, k):
         peer, length, keep, give = halves[k][s]
-        src = pack.at[pl.ds(al(base(st, k) + give), length)]
+        src = packed(st, k, gives[k][s], length)
         return remote(src, (r0, r1)[s].at[st, k], sent.at[st], rs_recv.at[st, s, k], peer)
 
     def gathered(st, k, row, rows):
-        if st == 0:
-            return kg.at[core, pl.ds(al(base(0, k) + row), rows)]
-        sup, m = UNITS[st][k // 2]
-        return kfull.at[pl.ds(al(sup * BLK + row), rows), pl.ds(al((4 * m + 2 * core + k % 2) * TILE, TILE), TILE)]
+        if st < 2:
+            return kg.at[core, pl.ds(base(st, k) + row, rows)]
+        sup, m = UNITS[st // 2][k // 2]
+        return kfull.at[pl.ds(sup * BLK + st % 2 * HALF + row, rows), pl.ds(columns[m][k % 2], TILE)]
 
     def x_copies(st, e, k):
         d1, d2, d3 = dims(k)
@@ -172,7 +175,7 @@
         cps = []
         for j in PEERS:
             if e == 0:
-                src = pack.at[pl.ds(al(quarter(st, k) + pieces[k][j]), OWN)]
+                src = packed(st, k, pieces[k][j], OWN)
                 dst = r2.at[st, k, j - 1]
             else:
                 src = dst = r3.at[st, k, coords[dim]]
@@ -181,25 +184,25 @@
 
     def gather_copies(st, k, j):
         d1, d2, d3 = dims(k)
-        ref = gathered(st, k, halves[k][1][2] + pieces[k][(4 - j) % 4], OWN)
+        ref = gathered(st, k, pieces[k][(4 - j) % 4], OWN)
         cps = [remote(ref, ref, sent.at[st], far_recv.at[st, k, i - 1], ring[d1][i]) for i in PEERS]
         if j == 0:
             cps = [remote(ref, ref, sent.at[st], near_recv.at[st, k, i - 1], ring[d2][i]) for i in PEERS] + cps
         return cps
 
     def dd_copy(st, k, j):
-        ref = gathered(st, k, halves[k][1][2] if j == 0 else places[k][4 - j], TILE)
+        ref = gathered(st, k, keeps[k][1] if j == 0 else places[k][4 - j], QUARTER)
         return remote(ref, ref, sent.at[st], dd_recv.at[st, k], mate)
 
     def s_copies(ph, d):
         dim = ((d + 1) % 3, d)[ph]
         return [
-            remote(svec.at[ph, d], srecv.at[ph, d, j - 1], sent.at[2], s_recv.at[ph, d], ring[dim][j])
+            remote(svec.at[ph, d], srecv.at[ph, d, j - 1], sent.at[STREAMS - 1], s_recv.at[ph, d], ring[dim][j])
             for j in PEERS
         ]
 
     def sp_copy():
-        return remote(stot, spart, sent.at[2], sp_recv, mate)
+        return remote(stot, spart, sent.at[STREAMS - 1], sp_recv, mate)
 
     def products(m):
         mine = bfull[pl.ds(al(m * BLK + HALF * core), HALF), :]
@@ -226,28 +229,28 @@
             return nrow[pl.ds((4 * m + i) * TILE, TILE), :] + ncol[4 * m + j:4 * m + j + 1, :] - 2.0 * tile(i, j % 2)
 
         for t in range(3):
-            pack[pl.ds(base(0, m) + t * TILE, TILE), :] = jnp.where(core == 0, dist(*OFFS[0][t]), dist(*OFFS[1][t]))
+            pack[pl.ds(tile_row(0, m, t), TILE), :] = jnp.where(core == 0, dist(*OFFS[0][t]), dist(*OFFS[1][t]))
         one = jnp.where(core == 0, dist(0, 0), dist(2, 2))
         two = jnp.where(core == 0, dist(1, 1), dist(3, 3))
-        pack[pl.ds(base(0, m) + 3 * TILE, TILE), :] = jnp.where(upper, one, two)
-        begin([rs_copy(0, 0, m)])
-        for st in (1, 2):
-            for u, (sup, col) in enumerate(UNITS[st]):
+        pack[pl.ds(tile_row(0, m, 3), TILE), :] = jnp.where(upper, one, two)
+        begin([rs_copy(0, 0, m), rs_copy(1, 0, m)])
+        for kind in (1, 2):
+            for u, (sup, col) in enumerate(UNITS[kind]):
                 if col != m:
                     continue
                 for b in range(2):
                     nc = ncol[pl.ds(4 * m + 2 * core + b, 1), :]
                     for a in range(4):
                         nr = nrow[pl.ds((4 * sup + a) * TILE, TILE), :]
-                        pack[pl.ds(base(st, 2 * u + b) + a * TILE, TILE), :] = nr + nc - 2.0 * block(4 * sup + a, b)
-                begin([rs_copy(st, 0, 2 * u), rs_copy(st, 0, 2 * u + 1)])
+                        pack[pl.ds(tile_row(kind, 2 * u + b, a), TILE), :] = nr + nc - 2.0 * block(4 * sup + a, b)
+                begin([rs_copy(st, 0, 2 * u + b) for st in (2 * kind, 2 * kind + 1) for b in range(2)])
 
     def pm_tiles(half):
         for ch in (2 * half, 2 * half + 1):
             pre_pm(ch).wait_recv()
             mine = pl.ds(al(ch * BLK + core * HALF), HALF)
-            pack[pl.ds(PM_ROW + ch * HALF, HALF), :] = pml[mine, :] + pmr[pl.ds(ch * HALF, HALF), :]
-        begin([rs_copy(0, 0, 4 + half)])
+            pack[pl.ds(base(ch % 2, 4 + half), HALF), :] = pml[mine, :] + pmr[pl.ds(ch * HALF, HALF), :]
+            begin([rs_copy(ch % 2, 0, 4 + half)])
 
     def open_step():
         begin([pre_pm(3), pre_bf16(7)])
@@ -283,7 +286,7 @@
 
     def one_step(step_index, carry):
         def row_sums(st, k, kern):
-            place = own(0, k) - base(0, k)
+            place = pieces[k][0] + st % 2 * HALF
             slot, r = div(place, TILE), rem(place, TILE)
 
             def by_rows(vals):
@@ -293,8 +296,8 @@
             def by_cols(vals):
                 return jnp.sum(vals, axis=0, keepdims=True)
 
-            if st > 0:
-                sup, m = UNITS[st][k // 2]
+            if st > 1:
+                sup, m = UNITS[st // 2][k // 2]
                 return [(4 * sup + slot, by_rows(kern)), (4 * m + 2 * core + k % 2, by_cols(kern))]
             both = div(slot, 3)
             up_one = div(slot + 1, 2)
@@ -307,66 +310,67 @@
 
         def advance(st, s):
             parts = [[], [], []]
-            if st == 2 and s == 4:
+            if s == 4 and st == STREAMS - 1:
                 for d in range(3):
                     arrive(srecv.at[0, d], s_recv.at[0, d])
                     svec[1, d] = svec[0, d] + srecv[0, d, 0] + srecv[0, d, 1] + srecv[0, d, 2]
                     begin(s_copies(1, d))
-            if st == 2 and s == 5:
+            if s == 5 and st == STREAMS - 1:
                 tot = jnp.zeros((16, TILE), F32)
                 for d in range(3):
                     arrive(srecv.at[1, d], s_recv.at[1, d])
                     tot = tot + ((svec[1, d] + srecv[1, d, 0]) + (srecv[1, d, 1] + srecv[1, d, 2]))
                 stot[...] = tot
                 begin([sp_copy()])
-            for k in range(COLORS):
-                mine = pl.ds(al(own(st, k)), OWN)
+            kerns = []
+            for k in range(COLORS if s < 4 else 0):
                 if s < 2:
                     peer, length, keep, give = halves[k][s]
                     rs_copy(st, s, k).wait_recv()
-                    rng = pl.ds(al(base(st, k) + keep), length)
-                    pack[rng, :] += (r0, r1)[s][st, k]
+                    packed(st, k, keeps[k][s], length)[...] += (r0, r1)[s][st, k]
                     begin([rs_copy(st, 1, k)] if s == 0 else x_copies(st, 0, k))
                 elif s == 2:
                     x_arrive(st, 0, k)
-                    r3[st, k, coords[dims(k)[2]]] = pack[mine, :] + r2[st, k, 0] + r2[st, k, 1] + r2[st, k, 2]
+                    r3[st, k, coords[dims(k)[2]]] = packed(st, k, pieces[k][0], OWN)[...] + r2[st, k, 0] + r2[st, k, 1] + r2[st, k, 2]
                     begin(x_copies(st, 1, k))
-                elif s == 3:
+                else:
                     x_arrive(st, 1, k)
                     full = (r3[st, k, 0] + r3[st, k, 1]) + (r3[st, k, 2] + r3[st, k, 3])
-                    if st == 0 and k >= 4:
-                        kern = full
-                    else:
-                        kern = jnp.exp(-jnp.maximum(full, 0.0) / bandwidth)
-                        parts[k % 3] += row_sums(st, k, kern)
-                    gathered(st, k, own(0, k) - base(0, k), OWN)[...] = kern.astype(BF16)
+                    kern = full if st < 2 and k >= 4 else jnp.exp(-jnp.maximum(full, 0.0) / bandwidth)
+                    gathered(st, k, pieces[k][0], OWN)[...] = kern.astype(BF16)
                     begin(gather_copies(st, k, 0))
-                elif s == 4:
-                    for j in PEERS:
+                    kerns.append(kern)
+            for j in NEAR_FIRST if s >= 4 else ():
+                for k in range(COLORS):
+                    if s == 4:
                         arrive(kg.at[core, 0:OWN], near_recv.at[st, k, j - 1])
                         begin(gather_copies(st, k, j))
-                    begin([dd_copy(st, k, 0)])
-                else:
-                    for j in PEERS:
-                        arrive(kg.at[core, 0:TILE], far_recv.at[st, k, j - 1])
+                        if j == NEAR_FIRST[-1]:
+                            begin([dd_copy(st, k, 0)])
+                    else:
+                        arrive(kg.at[core, 0:QUARTER], far_recv.at[st, k, j - 1])
                         begin([dd_copy(st, k, j)])
             if s == 3:
+                for k, kern in enumerate(kerns):
+                    if st > 1 or k < 4:
+                        parts[k % 3] += row_sums(st, k, kern)
                 for d in range(3):
                     if st == 0:
                         svec[0, d] = jnp.zeros((16, TILE), F32)
                     for block, line in parts[d]:
                         svec[0, d, pl.ds(block, 1), :] += line
-                    if st == 2:
+                    if st == STREAMS - 1:
                         begin(s_copies(0, d))
-        def unpack_wait(st):
-            for k in range(COLORS):
-                arrive(kg.at[core, 0:BLK], dd_recv.at[st, k])
-
-        def unpack(st):
+        def unpack_wait(kind):
+            for st in (2 * kind, 2 * kind + 1):
+                for k in range(COLORS):
+                    arrive(kg.at[core, 0:HALF], dd_recv.at[st, k])
+
+        def unpack(kind):
             for c in range(2):
-                if st > 0:
+                if kind > 0:
                     for k in range(COLORS):
-                        sup, m = UNITS[st][k // 2]
+                        sup, m = UNITS[kind][k // 2]
                         jrng = pl.ds((4 * m + 2 * c + k % 2) * TILE, TILE)
                         for a in range(4):
                             srng = pl.ds((4 * sup + a) * TILE, TILE)
@@ -374,11 +378,11 @@
                     continue
                 for sup in range(4):
                     for t, (i, j) in enumerate(OFFS[c]):
-                        src = kg[c, pl.ds(base(0, sup) + t * TILE, TILE), :]
+                        src = kg[c, pl.ds(tile_row(0, sup, t), TILE), :]
                         ri, rj = pl.ds((4 * sup + i) * TILE, TILE), pl.ds((4 * sup + j) * TILE, TILE)
                         kfull[ri, rj] = src
                         kfull[rj, ri] = src.T
-                    src = kg[c, pl.ds(base(0, sup) + 3 * TILE, TILE), :]
+                    src = kg[c, pl.ds(tile_row(0, sup, 3), TILE), :]
                     srt = src.T
                     one = jnp.ones((TILE, TILE), BF16)
                     ra, rb = pl.ds((4 * sup + 2 * c) * TILE, TILE), pl.ds((4 * sup + 2 * c + 1) * TILE, TILE)
@@ -395,7 +399,8 @@
         def drive():
             for q in range(8):
                 rows = pl.ds(q * HALF, HALF)
-                pm = kg[q % 2, pl.ds(PM_ROW + (q // 2) * HALF, HALF), :]
+                ch = q // 2
+                pm = kg[q % 2, pl.ds(base(ch % 2, 4 + ch // 2), HALF), :]
                 low = lax.dot_general(pm, fac_ref[...], NT, preferred_element_type=F32)
                 adrv[rows, :] = ((pulled[rows, :] + low) + scaled[rows, :]).astype(BF16)
 
@@ -428,20 +433,27 @@
                 begin([pre_bf16(start // HALF)])
 
         drive_parts()
-        for s in range(5):
-            for st in range(3):
+        def early_rounds(s):
+            def one(st, c):
                 advance(st, s)
-        advance(0, 5)
-        advance(1, 5)
-        unpack_wait(0)
-        unpack(0)
-        drive()
-        advance(2, 5)
+                return c
+
+            lax.fori_loop(0, STREAMS, one, 0)
+
+        for s in range(3):
+            early_rounds(s)
+        for s in range(3, 6):
+            for st in range(STREAMS):
+                if s == 5 and st == STREAMS - 2:
+                    unpack_wait(0)
+                    unpack(0)
+                    drive()
+                advance(st, s)
         remote(pack.at[0:5120], pack.at[0:5120], pre_send, sp_recv, mate).wait_send()
-        def update(starts, st):
+        def update(starts, kind):
             tot = stot[...] + spart[...] + 1.0
             ahead = product(starts[0])
-            unpack(st)
+            unpack(kind)
             held = []
             for n, start in enumerate(starts):
                 acc = ahead
@@ -457,8 +469,8 @@
         update(range(0, BLK, HALF), 1)
         unpack_wait(2)
         update(range(BLK, ROWS, HALF), 2)
-        for st in range(3):
-            total = pack.at[0:SENT + (SENT_SUMS if st == 2 else 0)]
+        for st in range(STREAMS):
+            total = pack.at[0:SENT + (SENT_SUMS if st == STREAMS - 1 else 0)]
             remote(total, total, sent.at[st], sp_recv, mate).wait_send()
         pl.when(step_index < NUM_STEPS - 1)(open_step)
         return carry
@@ -494,11 +506,12 @@
                     vm((ROWS, 2 * loc), BF16), vm((ROWS, rank), F32), vm((ROWS // 2, rank), F32),
                     vm((ROWS, TILE), F32), vm((16, TILE), F32), vm((ROWS, loc), F32), vm((ROWS, loc), F32),
                     vm((3 * SROWS, TILE), F32),
-                    vm((3, COLORS, BLK // 2, TILE), F32), vm((3, COLORS, BLK // 4, TILE), F32),
-                    vm((3, COLORS, 3, OWN, TILE), F32), vm((3, COLORS, 4, OWN, TILE), F32),
+                    vm((STREAMS, COLORS, HALF // 2, TILE), F32), vm((STREAMS, COLORS, QUARTER, TILE), F32),
+                    vm((STREAMS, COLORS, 3, OWN, TILE), F32), vm((STREAMS, COLORS, 4, OWN, TILE), F32),
                     vm((2, SROWS, TILE), BF16), vm((ROWS, ROWS), BF16), vm((ROWS, loc), BF16),
                     vm((2, 3, 16, TILE), F32), vm((2, 3, 3, 16, TILE), F32), vm((16, TILE), F32), vm((16, TILE), F32),
-                    dma((7,)), dma, dma((12,)), dma((3,)), dma((3, 2, COLORS)), dma((3, 2, COLORS)), dma((3, COLORS, 3)), dma((3, COLORS, 3)), dma((3, COLORS)),
+                    dma((7,)), dma, dma((12,)), dma((STREAMS,)), dma((STREAMS, 2, COLORS)), dma((STREAMS, 2, COLORS)),
+                    dma((STREAMS, COLORS, 3)), dma((STREAMS, COLORS, 3)), dma((STREAMS, COLORS)),
                     dma((2, 3)), dma,
                 ],
                 compiler_params=pltpu.CompilerParams(collective_id=0, has_side_effects=True, vmem_limit_bytes=50000000),

time: 149 us -> 149 us (level)
  no operation moved by 1% of the time
where the time goes in v10:
time: 149 us
  Pallas kernels  147 us (99%)
  local copies, waits for them, and re-layouts  2.02 us (1%)
    pallas_call x1, Pallas kernels, local_steps(): call(hbm(current), hbm(prec_loc.reshape(1, loc)), hbm(mean_loc.reshape(1,...  147 us

profile of v10, /device:TPU:1, one launch (start us, length us, event | category | flops | bytes accessed | tf_op | source)
XLA Modules:
  0.0 148.6 jit_solution(5095969439661088047)
XLA Ops:
  0.0 146.6 %svgd.1 = f32[2048,512]{1,0:T(8,128)S(1)} custom-call(f32[2048,512]{1,0:T(8,128)} %theta_ref.1, f32[1,512]{1,0:T(1,128)} %bitcast.2, f32[1,512]{1,0:T(1,128)} %bitcast.3, bf16[512,128]{1,0:T(8,128)(2,1)} %fac_hbm.1), custom_call_target="tpu_custom_call" | custom-call | tf_op jit(solution)/shard_map/svgd/pallas_call | solution.py:521
  146.6 2.0 %copy.6 = f32[2048,512]{1,0:T(8,128)} copy(f32[2048,512]{1,0:T(8,128)S(1)} %svgd.1) | data formatting | bytes 8388608

commit v11 on v10

--- a/solution.py
+++ b/solution.py
@@ -110,17 +110,19 @@
     def packed(st, k, row, rows):
         return pack.at[pl.ds(al(base(st, k) + row), rows)]
 
+    loads = [pltpu.make_async_copy(theta_ref.at[pl.ds(ch * BLK, BLK)], out_ref.at[pl.ds(ch * BLK, BLK)], in_sem.at[ch]) for ch in range(4)]
+    loads += [
+        pltpu.make_async_copy(src, dst, in_sem.at[4 + n])
+        for n, (src, dst) in enumerate(((mu_hbm, mu_ref), (fac_hbm, fac_ref), (lam_hbm, lam_ref)))
+    ]
+    for cp in loads[4:] + loads[:1]:
+        cp.start()
     barrier = pltpu.get_barrier_semaphore()
     pl.semaphore_signal(barrier, inc=1, device_id=mate, device_id_type=MESH)
     for dim in range(3):
         for j in PEERS:
             pl.semaphore_signal(barrier, inc=1, device_id=ring[dim][j], device_id_type=MESH)
-    loads = [pltpu.make_async_copy(theta_ref.at[pl.ds(ch * BLK, BLK)], out_ref.at[pl.ds(ch * BLK, BLK)], in_sem.at[ch]) for ch in range(4)]
-    loads += [
-        pltpu.make_async_copy(src, dst, in_sem.at[4 + n])
-        for n, (src, dst) in enumerate(((mu_hbm, mu_ref), (fac_hbm, fac_ref), (lam_hbm, lam_ref)))
-    ]
-    for cp in loads[4:] + loads[:4]:
+    for cp in loads[1:4]:
         cp.start()
 
     row_i = lax.broadcasted_iota(jnp.int32, (TILE, TILE), 0)
@@ -155,8 +157,8 @@
     def arrive(ref, sem):
         remote(ref, ref, sent.at[0], sem, mate).wait_recv()
 
-    def x_arrive(st, e, k):
-        arrive((r2.at[st, k], r3.at[st, k, 0:3])[e], x_recv.at[st, e, k])
+    def pair_arrive(rows, sem):
+        arrive(pack.at[0:6 * rows], sem)
 
     def rs_copy(st, s, k):
         peer, length, keep, give = halves[k][s]
@@ -179,20 +181,20 @@
                 dst = r2.at[st, k, j - 1]
             else:
                 src = dst = r3.at[st, k, coords[dim]]
-            cps.append(remote(src, dst, sent.at[st], x_recv.at[st, e, k], ring[dim][j]))
+            cps.append(remote(src, dst, sent.at[st], x_recv.at[st, e, k % 3], ring[dim][j]))
         return cps
 
     def gather_copies(st, k, j):
         d1, d2, d3 = dims(k)
         ref = gathered(st, k, pieces[k][(4 - j) % 4], OWN)
-        cps = [remote(ref, ref, sent.at[st], far_recv.at[st, k, i - 1], ring[d1][i]) for i in PEERS]
+        cps = [remote(ref, ref, sent.at[st], far_recv.at[st, k % 3], ring[d1][i]) for i in PEERS]
         if j == 0:
-            cps = [remote(ref, ref, sent.at[st], near_recv.at[st, k, i - 1], ring[d2][i]) for i in PEERS] + cps
+            cps = [remote(ref, ref, sent.at[st], near_recv.at[st, k % 3], ring[d2][i]) for i in PEERS] + cps
         return cps
 
     def dd_copy(st, k, j):
         ref = gathered(st, k, keeps[k][1] if j == 0 else places[k][4 - j], QUARTER)
-        return remote(ref, ref, sent.at[st], dd_recv.at[st, k], mate)
+        return remote(ref, ref, sent.at[st], dd_recv.at[st], mate)
 
     def s_copies(ph, d):
         dim = ((d + 1) % 3, d)[ph]
@@ -252,15 +254,15 @@
             pack[pl.ds(base(ch % 2, 4 + half), HALF), :] = pml[mine, :] + pmr[pl.ds(ch * HALF, HALF), :]
             begin([rs_copy(ch % 2, 0, 4 + half)])
 
-    def open_step():
-        begin([pre_pm(3), pre_bf16(7)])
+    def open_step(finish_last):
         pm_tiles(0)
         for piece in range(4):
             pre_bf16(piece).wait_recv()
-        gs = []
+        gs = [products(m) for m in range(2)]
+        finish_last()
         for m in range(2):
-            gs.append(products(m))
             norms(m)
+        begin([pre_pm(3), pre_bf16(7)])
         for m in range(2):
             tiles(m, gs[m])
         pm_tiles(1)
@@ -282,7 +284,7 @@
         if ch < 3:
             begin([pre_pm(ch)])
         begin([pre_bf16(piece) for piece in (2 * ch, 2 * ch + 1) if piece < 7])
-    open_step()
+    open_step(lambda: None)
 
     def one_step(step_index, carry):
         def row_sums(st, k, kern):
@@ -322,36 +324,34 @@
                     tot = tot + ((svec[1, d] + srecv[1, d, 0]) + (srecv[1, d, 1] + srecv[1, d, 2]))
                 stot[...] = tot
                 begin([sp_copy()])
-            kerns = []
-            for k in range(COLORS if s < 4 else 0):
+            kerns = {}
+            for k in (range(COLORS) if s < 2 else (0, 3, 1, 4, 2, 5)):
                 if s < 2:
                     peer, length, keep, give = halves[k][s]
                     rs_copy(st, s, k).wait_recv()
                     packed(st, k, keeps[k][s], length)[...] += (r0, r1)[s][st, k]
                     begin([rs_copy(st, 1, k)] if s == 0 else x_copies(st, 0, k))
-                elif s == 2:
-                    x_arrive(st, 0, k)
+                    continue
+                if k < 3:
+                    sem = x_recv.at[st, s - 2, k] if s < 4 else (near_recv, far_recv)[s - 4].at[st, k]
+                    pair_arrive((OWN, OWN, OWN // 2, QUARTER // 2)[s - 2], sem)
+                if s == 2:
                     r3[st, k, coords[dims(k)[2]]] = packed(st, k, pieces[k][0], OWN)[...] + r2[st, k, 0] + r2[st, k, 1] + r2[st, k, 2]
                     begin(x_copies(st, 1, k))
-                else:
-                    x_arrive(st, 1, k)
+                elif s == 3:
                     full = (r3[st, k, 0] + r3[st, k, 1]) + (r3[st, k, 2] + r3[st, k, 3])
                     kern = full if st < 2 and k >= 4 else jnp.exp(-jnp.maximum(full, 0.0) / bandwidth)
                     gathered(st, k, pieces[k][0], OWN)[...] = kern.astype(BF16)
                     begin(gather_copies(st, k, 0))
-                    kerns.append(kern)
-            for j in NEAR_FIRST if s >= 4 else ():
-                for k in range(COLORS):
-                    if s == 4:
-                        arrive(kg.at[core, 0:OWN], near_recv.at[st, k, j - 1])
+                    kerns[k] = kern
+                elif s == 4:
+                    begin([dd_copy(st, k, 0)])
+                    for j in NEAR_FIRST:
                         begin(gather_copies(st, k, j))
-                        if j == NEAR_FIRST[-1]:
-                            begin([dd_copy(st, k, 0)])
-                    else:
-                        arrive(kg.at[core, 0:QUARTER], far_recv.at[st, k, j - 1])
-                        begin([dd_copy(st, k, j)])
+                else:
+                    begin([dd_copy(st, k, j) for j in NEAR_FIRST])
             if s == 3:
-                for k, kern in enumerate(kerns):
+                for k, kern in kerns.items():
                     if st > 1 or k < 4:
                         parts[k % 3] += row_sums(st, k, kern)
                 for d in range(3):
@@ -363,8 +363,7 @@
                         begin(s_copies(0, d))
         def unpack_wait(kind):
             for st in (2 * kind, 2 * kind + 1):
-                for k in range(COLORS):
-                    arrive(kg.at[core, 0:HALF], dd_recv.at[st, k])
+                arrive(kg.at[core, 0:COLORS * HALF], dd_recv.at[st])
 
         def unpack(kind):
             for c in range(2):
@@ -461,6 +460,8 @@
                     ahead = product(starts[n + 1])
                 if n:
                     share(starts[n - 1])
+                if start + HALF == ROWS:
+                    return lambda: finish(start, acc, tot, list(held))
                 finish(start, acc, tot, held)
             share(starts[-1])
 
@@ -468,11 +469,12 @@
         arrive(stot, sp_recv)
         update(range(0, BLK, HALF), 1)
         unpack_wait(2)
-        update(range(BLK, ROWS, HALF), 2)
+        finish_last = update(range(BLK, ROWS, HALF), 2)
         for st in range(STREAMS):
             total = pack.at[0:SENT + (SENT_SUMS if st == STREAMS - 1 else 0)]
             remote(total, total, sent.at[st], sp_recv, mate).wait_send()
-        pl.when(step_index < NUM_STEPS - 1)(open_step)
+        pl.when(step_index < NUM_STEPS - 1)(lambda: open_step(finish_last))
+        pl.when(step_index == NUM_STEPS - 1)(finish_last)
         return carry
 
     lax.fori_loop(0, NUM_STEPS, one_step, 0)
@@ -510,8 +512,8 @@
                     vm((STREAMS, COLORS, 3, OWN, TILE), F32), vm((STREAMS, COLORS, 4, OWN, TILE), F32),
                     vm((2, SROWS, TILE), BF16), vm((ROWS, ROWS), BF16), vm((ROWS, loc), BF16),
                     vm((2, 3, 16, TILE), F32), vm((2, 3, 3, 16, TILE), F32), vm((16, TILE), F32), vm((16, TILE), F32),
-                    dma((7,)), dma, dma((12,)), dma((STREAMS,)), dma((STREAMS, 2, COLORS)), dma((STREAMS, 2, COLORS)),
-                    dma((STREAMS, COLORS, 3)), dma((STREAMS, COLORS, 3)), dma((STREAMS, COLORS)),
+                    dma((7,)), dma, dma((12,)), dma((STREAMS,)), dma((STREAMS, 2, COLORS)), dma((STREAMS, 2, 3)),
+                    dma((STREAMS, 3)), dma((STREAMS, 3)), dma((STREAMS,)),
                     dma((2, 3)), dma,
                 ],
                 compiler_params=pltpu.CompilerParams(collective_id=0, has_side_effects=True, vmem_limit_bytes=50000000),

time: 149 us -> 148 us (level)
  no operation moved by 1% of the time
where the time goes in v11:
time: 148 us
  Pallas kernels  146 us (99%)
  local copies, waits for them, and re-layouts  2.02 us (1%)
    pallas_call x1, Pallas kernels, local_steps(): call(hbm(current), hbm(prec_loc.reshape(1, loc)), hbm(mean_loc.reshape(1,...  146 us

profile of v11, /device:TPU:1, one launch (start us, length us, event | category | flops | bytes accessed | tf_op | source)
XLA Modules:
  0.0 148.1 jit_solution(5026236174365791786)
XLA Ops:
  0.0 146.1 %svgd.1 = f32[2048,512]{1,0:T(8,128)S(1)} custom-call(f32[2048,512]{1,0:T(8,128)} %theta_ref.1, f32[1,512]{1,0:T(1,128)} %bitcast.2, f32[1,512]{1,0:T(1,128)} %bitcast.3, bf16[512,128]{1,0:T(8,128)(2,1)} %fac_hbm.1), custom_call_target="tpu_custom_call" | custom-call | tf_op jit(solution)/shard_map/svgd/pallas_call | solution.py:523
  146.1 2.0 %copy.6 = f32[2048,512]{1,0:T(8,128)} copy(f32[2048,512]{1,0:T(8,128)S(1)} %svgd.1) | data formatting | bytes 8388608

commit v12 on v11

--- a/solution.py
+++ b/solution.py
@@ -258,9 +258,10 @@
         pm_tiles(0)
         for piece in range(4):
             pre_bf16(piece).wait_recv()
-        gs = [products(m) for m in range(2)]
         finish_last()
+        gs = []
         for m in range(2):
+            gs.append(products(m))
             norms(m)
         begin([pre_pm(3), pre_bf16(7)])
         for m in range(2):

time: 148 us -> 148 us (level)
  no operation moved by 1% of the time
where the time goes in v12:
time: 148 us
  Pallas kernels  146 us (99%)
  local copies, waits for them, and re-layouts  2.02 us (1%)
    pallas_call x1, Pallas kernels, local_steps(): call(hbm(current), hbm(prec_loc.reshape(1, loc)), hbm(mean_loc.reshape(1,...  146 us

profile of v12, /device:TPU:1, one launch (start us, length us, event | category | flops | bytes accessed | tf_op | source)
XLA Modules:
  0.0 147.9 jit_solution(3371862612116849323)
XLA Ops:
  0.0 145.9 %svgd.1 = f32[2048,512]{1,0:T(8,128)S(1)} custom-call(f32[2048,512]{1,0:T(8,128)} %theta_ref.1, f32[1,512]{1,0:T(1,128)} %bitcast.2, f32[1,512]{1,0:T(1,128)} %bitcast.3, bf16[512,128]{1,0:T(8,128)(2,1)} %fac_hbm.1), custom_call_target="tpu_custom_call" | custom-call | tf_op jit(solution)/shard_map/svgd/pallas_call | solution.py:524
  145.9 2.0 %copy.6 = f32[2048,512]{1,0:T(8,128)} copy(f32[2048,512]{1,0:T(8,128)S(1)} %svgd.1) | data formatting | bytes 8388608

commit v13 on v12

--- a/solution.py
+++ b/solution.py
@@ -19,6 +19,7 @@
 BLK = 2 * HALF
 COLORS = 6
 SROWS = COLORS * BLK
+PM_AT = ((0, 4), (1, 3), (0, 5), (1, 5))
 STREAMS = 6
 QUARTER = HALF // 4
 UNITS = ((), ((0, 3), (0, 1), (0, 2)), ((1, 2), (1, 3), (2, 3)))
@@ -91,11 +92,14 @@
     def dims(k):
         return k % 3, (k + 1) % 3, (k + 2) % 3
 
+    def moved(m, part):
+        return 4 if m == 3 and part == 1 else m
+
     def base(st, k):
         return (st * COLORS + k) * HALF
 
     def tile_row(kind, k, a):
-        return base(2 * kind + a // 2, k) + a % 2 * TILE
+        return base(2 * kind + a // 2, moved(k, a // 2) if kind == 0 else k) + a % 2 * TILE
 
     keeps = [[al(step[2]) for step in steps] for steps in halves]
     gives = [[al(step[3]) for step in steps] for steps in halves]
@@ -235,7 +239,7 @@
         one = jnp.where(core == 0, dist(0, 0), dist(2, 2))
         two = jnp.where(core == 0, dist(1, 1), dist(3, 3))
         pack[pl.ds(tile_row(0, m, 3), TILE), :] = jnp.where(upper, one, two)
-        begin([rs_copy(0, 0, m), rs_copy(1, 0, m)])
+        begin([rs_copy(part, 0, moved(m, part)) for part in range(2)])
         for kind in (1, 2):
             for u, (sup, col) in enumerate(UNITS[kind]):
                 if col != m:
@@ -247,15 +251,15 @@
                         pack[pl.ds(tile_row(kind, 2 * u + b, a), TILE), :] = nr + nc - 2.0 * block(4 * sup + a, b)
                 begin([rs_copy(st, 0, 2 * u + b) for st in (2 * kind, 2 * kind + 1) for b in range(2)])
 
-    def pm_tiles(half):
-        for ch in (2 * half, 2 * half + 1):
+    def pm_tiles(chs):
+        for ch in chs:
             pre_pm(ch).wait_recv()
             mine = pl.ds(al(ch * BLK + core * HALF), HALF)
-            pack[pl.ds(base(ch % 2, 4 + half), HALF), :] = pml[mine, :] + pmr[pl.ds(ch * HALF, HALF), :]
-            begin([rs_copy(ch % 2, 0, 4 + half)])
+            pack[pl.ds(base(*PM_AT[ch]), HALF), :] = pml[mine, :] + pmr[pl.ds(ch * HALF, HALF), :]
+            begin([rs_copy(PM_AT[ch][0], 0, PM_AT[ch][1])])
 
     def open_step(finish_last):
-        pm_tiles(0)
+        pm_tiles(range(3))
         for piece in range(4):
             pre_bf16(piece).wait_recv()
         finish_last()
@@ -266,7 +270,7 @@
         begin([pre_pm(3), pre_bf16(7)])
         for m in range(2):
             tiles(m, gs[m])
-        pm_tiles(1)
+        pm_tiles((3,))
         for m in range(2, 4):
             for piece in range(2 * m, 2 * m + 2):
                 pre_bf16(piece).wait_recv()
@@ -302,14 +306,15 @@
             if st > 1:
                 sup, m = UNITS[st // 2][k // 2]
                 return [(4 * sup + slot, by_rows(kern)), (4 * m + 2 * core + k % 2, by_cols(kern))]
+            m = min(k, 3)
             both = div(slot, 3)
             up_one = div(slot + 1, 2)
             i0 = (1 - both) * ((1 - core) * (slot + up_one) + core * (1 + div(slot, 2))) + both * 2 * core
             j0 = (1 - both) * ((1 - core) * (1 - up_one) + core * (2 + up_one)) + both * 2 * core
             up = jnp.where(lane_o + 1000 * (1 - both) > sub_o + r, kern, 0.0)
             lo = jnp.where(lane_o + 1000 * (1 - both) < sub_o + r, kern, 0.0)
-            nxt = 4 * k + 2 * core + 1
-            return [(4 * k + i0, by_rows(up)), (4 * k + j0, by_cols(up)), (nxt, by_rows(lo)), (nxt, by_cols(lo))]
+            nxt = 4 * m + 2 * core + 1
+            return [(4 * m + i0, by_rows(up)), (4 * m + j0, by_cols(up)), (nxt, by_rows(lo)), (nxt, by_cols(lo))]
 
         def advance(st, s):
             parts = [[], [], []]
@@ -341,7 +346,7 @@
                     begin(x_copies(st, 1, k))
                 elif s == 3:
                     full = (r3[st, k, 0] + r3[st, k, 1]) + (r3[st, k, 2] + r3[st, k, 3])
-                    kern = full if st < 2 and k >= 4 else jnp.exp(-jnp.maximum(full, 0.0) / bandwidth)
+                    kern = full if (st, k) in PM_AT else jnp.exp(-jnp.maximum(full, 0.0) / bandwidth)
                     gathered(st, k, pieces[k][0], OWN)[...] = kern.astype(BF16)
                     begin(gather_copies(st, k, 0))
                     kerns[k] = kern
@@ -353,7 +358,7 @@
                     begin([dd_copy(st, k, j) for j in NEAR_FIRST])
             if s == 3:
                 for k, kern in kerns.items():
-                    if st > 1 or k < 4:
+                    if (st, k) not in PM_AT:
                         parts[k % 3] += row_sums(st, k, kern)
                 for d in range(3):
                     if st == 0:
@@ -400,7 +405,7 @@
             for q in range(8):
                 rows = pl.ds(q * HALF, HALF)
                 ch = q // 2
-                pm = kg[q % 2, pl.ds(base(ch % 2, 4 + ch // 2), HALF), :]
+                pm = kg[q % 2, pl.ds(base(*PM_AT[ch]), HALF), :]
                 low = lax.dot_general(pm, fac_ref[...], NT, preferred_element_type=F32)
                 adrv[rows, :] = ((pulled[rows, :] + low) + scaled[rows, :]).astype(BF16)
 

time: 148 us -> 147 us (level)
  no operation moved by 1% of the time
where the time goes in v13:
time: 147 us
  Pallas kernels  145 us (99%)
  local copies, waits for them, and re-layouts  2.02 us (1%)
    pallas_call x1, Pallas kernels, local_steps(): call(hbm(current), hbm(prec_loc.reshape(1, loc)), hbm(mean_loc.reshape(1,...  145 us

profile of v13, /device:TPU:1, one launch (start us, length us, event | category | flops | bytes accessed | tf_op | source)
XLA Modules:
  0.0 147.1 jit_solution(13001288978618983120)
XLA Ops:
  0.0 145.1 %svgd.1 = f32[2048,512]{1,0:T(8,128)S(1)} custom-call(f32[2048,512]{1,0:T(8,128)} %theta_ref.1, f32[1,512]{1,0:T(1,128)} %bitcast.2, f32[1,512]{1,0:T(1,128)} %bitcast.3, bf16[512,128]{1,0:T(8,128)(2,1)} %fac_hbm.1), custom_call_target="tpu_custom_call" | custom-call | tf_op jit(solution)/shard_map/svgd/pallas_call | solution.py:529
  145.1 2.0 %copy.6 = f32[2048,512]{1,0:T(8,128)} copy(f32[2048,512]{1,0:T(8,128)S(1)} %svgd.1) | data formatting | bytes 8388608

commit v14 on v13

--- a/solution.py
+++ b/solution.py
@@ -19,7 +19,8 @@
 BLK = 2 * HALF
 COLORS = 6
 SROWS = COLORS * BLK
-PM_AT = ((0, 4), (1, 3), (0, 5), (1, 5))
+PM_AT = ((0, 0), (0, 1), (0, 5), (1, 5))
+DIAG_AT = (((1, 0), (1, 1)), ((0, 4), (1, 4)), ((0, 2), (0, 3)), ((1, 2), (1, 3)))
 STREAMS = 6
 QUARTER = HALF // 4
 UNITS = ((), ((0, 3), (0, 1), (0, 2)), ((1, 2), (1, 3), (2, 3)))
@@ -92,14 +93,12 @@
     def dims(k):
         return k % 3, (k + 1) % 3, (k + 2) % 3
 
-    def moved(m, part):
-        return 4 if m == 3 and part == 1 else m
-
     def base(st, k):
         return (st * COLORS + k) * HALF
 
     def tile_row(kind, k, a):
-        return base(2 * kind + a // 2, moved(k, a // 2) if kind == 0 else k) + a % 2 * TILE
+        st, k = DIAG_AT[k][a // 2] if kind == 0 else (2 * kind + a // 2, k)
+        return base(st, k) + a % 2 * TILE
 
     keeps = [[al(step[2]) for step in steps] for steps in halves]
     gives = [[al(step[3]) for step in steps] for steps in halves]
@@ -239,7 +238,7 @@
         one = jnp.where(core == 0, dist(0, 0), dist(2, 2))
         two = jnp.where(core == 0, dist(1, 1), dist(3, 3))
         pack[pl.ds(tile_row(0, m, 3), TILE), :] = jnp.where(upper, one, two)
-        begin([rs_copy(part, 0, moved(m, part)) for part in range(2)])
+        begin([rs_copy(st, 0, k) for st, k in DIAG_AT[m]])
         for kind in (1, 2):
             for u, (sup, col) in enumerate(UNITS[kind]):
                 if col != m:
@@ -263,13 +262,12 @@
         for piece in range(4):
             pre_bf16(piece).wait_recv()
         finish_last()
-        gs = []
+        one, zero = products(1), products(0)
         for m in range(2):
-            gs.append(products(m))
             norms(m)
         begin([pre_pm(3), pre_bf16(7)])
-        for m in range(2):
-            tiles(m, gs[m])
+        tiles(1, one)
+        tiles(0, zero)
         pm_tiles((3,))
         for m in range(2, 4):
             for piece in range(2 * m, 2 * m + 2):
@@ -293,7 +291,8 @@
 
     def one_step(step_index, carry):
         def row_sums(st, k, kern):
-            place = pieces[k][0] + st % 2 * HALF
+            m, part = (0, st % 2) if st > 1 else [(m, part) for m in range(4) for part in range(2) if DIAG_AT[m][part] == (st, k)][0]
+            place = pieces[k][0] + part * HALF
             slot, r = div(place, TILE), rem(place, TILE)
 
             def by_rows(vals):
@@ -306,7 +305,6 @@
             if st > 1:
                 sup, m = UNITS[st // 2][k // 2]
                 return [(4 * sup + slot, by_rows(kern)), (4 * m + 2 * core + k % 2, by_cols(kern))]
-            m = min(k, 3)
             both = div(slot, 3)
             up_one = div(slot + 1, 2)
             i0 = (1 - both) * ((1 - core) * (slot + up_one) + core * (1 + div(slot, 2))) + both * 2 * core

time: 147 us -> 146 us (level)
    pallas_call x1, Pallas kernels: 145 us -> 144 us  [local_steps(): call(hbm(current), hbm(prec_loc.reshape(1, loc)), hbm(mean_loc.reshape(1,...]
where the time goes in v14:
time: 146 us
  Pallas kernels  144 us (99%)
  local copies, waits for them, and re-layouts  2.02 us (1%)
    pallas_call x1, Pallas kernels, local_steps(): call(hbm(current), hbm(prec_loc.reshape(1, loc)), hbm(mean_loc.reshape(1,...  144 us

profile of v14, /device:TPU:1, one launch (start us, length us, event | category | flops | bytes accessed | tf_op | source)
XLA Modules:
  0.0 145.6 jit_solution(4917410025323795231)
XLA Ops:
  0.0 143.5 %svgd.1 = f32[2048,512]{1,0:T(8,128)S(1)} custom-call(f32[2048,512]{1,0:T(8,128)} %theta_ref.1, f32[1,512]{1,0:T(1,128)} %bitcast.2, f32[1,512]{1,0:T(1,128)} %bitcast.3, bf16[512,128]{1,0:T(8,128)(2,1)} %fac_hbm.1), custom_call_target="tpu_custom_call" | custom-call | tf_op jit(solution)/shard_map/svgd/pallas_call | solution.py:527
  143.5 2.0 %copy.6 = f32[2048,512]{1,0:T(8,128)} copy(f32[2048,512]{1,0:T(8,128)S(1)} %svgd.1) | data formatting | bytes 8388608

commit v15 on v14

--- a/solution.py
+++ b/solution.py
@@ -261,20 +261,22 @@
         pm_tiles(range(3))
         for piece in range(4):
             pre_bf16(piece).wait_recv()
-        finish_last()
-        one, zero = products(1), products(0)
+        one = products(1)
         for m in range(2):
             norms(m)
+        zero = products(0)
+        tiles(1, one)
+        finish_last()
         begin([pre_pm(3), pre_bf16(7)])
-        tiles(1, one)
         tiles(0, zero)
-        pm_tiles((3,))
         for m in range(2, 4):
             for piece in range(2 * m, 2 * m + 2):
                 pre_bf16(piece).wait_recv()
             g = products(m)
             norms(m)
             tiles(m, g)
+            if m == 2:
+                pm_tiles((3,))
 
     for cp in loads[4:]:
         cp.wait()

time: 146 us -> 146 us (level)
  no operation moved by 1% of the time
where the time goes in v15:
time: 146 us
  Pallas kernels  144 us (99%)
  local copies, waits for them, and re-layouts  2.02 us (1%)
    pallas_call x1, Pallas kernels, local_steps(): call(hbm(current), hbm(prec_loc.reshape(1, loc)), hbm(mean_loc.reshape(1,...  144 us

profile of v15, /device:TPU:1, one launch (start us, length us, event | category | flops | bytes accessed | tf_op | source)
XLA Modules:
  0.0 146.1 jit_solution(8823949176375019079)
XLA Ops:
  0.0 144.1 %svgd.1 = f32[2048,512]{1,0:T(8,128)S(1)} custom-call(f32[2048,512]{1,0:T(8,128)} %theta_ref.1, f32[1,512]{1,0:T(1,128)} %bitcast.2, f32[1,512]{1,0:T(1,128)} %bitcast.3, bf16[512,128]{1,0:T(8,128)(2,1)} %fac_hbm.1), custom_call_target="tpu_custom_call" | custom-call | tf_op jit(solution)/shard_map/svgd/pallas_call | solution.py:529
  144.1 2.0 %copy.6 = f32[2048,512]{1,0:T(8,128)} copy(f32[2048,512]{1,0:T(8,128)S(1)} %svgd.1) | data formatting | bytes 8388608

commit v16 on v14

--- a/solution.py
+++ b/solution.py
@@ -47,7 +47,7 @@
     bandwidth, step_size, n_part,
     theta_ref, lam_hbm, mu_hbm, fac_hbm, out_ref,
     lam_ref, mu_ref, fac_ref,
-    bfull, pml, pmr, nrow, ncol, pulled, scaled, pack, r0, r1, r2, r3, kg, kfull, adrv, svec, srecv, stot, spart,
+    bfull, pml, pmr, nown, nrow, ncol, pulled, scaled, pack, r0, r1, r2, r3, kg, kfull, adrv, svec, srecv, stot, spart,
     in_sem, pre_send, pre_recv, sent, rs_recv, x_recv, near_recv, far_recv, dd_recv, s_recv, sp_recv,
 ):
     width = out_ref.shape[1]
@@ -146,7 +146,10 @@
         return remote(src, dst, pre_send, pre_recv.at[8 + ch], mate)
 
     def prepare(start, th):
-        bfull[pl.ds(start, HALF), 0:width] = th.astype(BF16)
+        rounded = th.astype(BF16)
+        bfull[pl.ds(start, HALF), 0:width] = rounded
+        wide = rounded.astype(F32)
+        nown[pl.ds(start, HALF), :] = jnp.broadcast_to(jnp.sum(wide * wide, axis=1, keepdims=True), (HALF, TILE))
         return (th - mu_ref[...]).astype(BF16)
 
     def partial_pm(start, centered):
@@ -217,8 +220,8 @@
     def norms(m):
         for i in range(4):
             rows = pl.ds((4 * m + i) * TILE, TILE)
-            wide = bfull[rows, :].astype(F32)
-            n = jnp.broadcast_to(jnp.sum(wide * wide, axis=1, keepdims=True), (TILE, TILE))
+            wide = bfull[rows, width:2 * width].astype(F32)
+            n = nown[rows, :] + jnp.sum(wide * wide, axis=1, keepdims=True)
             nrow[rows, :] = n
             ncol[4 * m + i:4 * m + i + 1, :] = jnp.sum(jnp.where(eye, n, 0.0), axis=0, keepdims=True)
 
@@ -509,7 +512,7 @@
                 out_specs=spec,
                 scratch_shapes=[
                     vm((1, loc), F32), vm((1, loc), F32), vm((loc, rank), BF16),
-                    vm((ROWS, 2 * loc), BF16), vm((ROWS, rank), F32), vm((ROWS // 2, rank), F32),
+                    vm((ROWS, 2 * loc), BF16), vm((ROWS, rank), F32), vm((ROWS // 2, rank), F32), vm((ROWS, TILE), F32),
                     vm((ROWS, TILE), F32), vm((16, TILE), F32), vm((ROWS, loc), F32), vm((ROWS, loc), F32),
                     vm((3 * SROWS, TILE), F32),
                     vm((STREAMS, COLORS, HALF // 2, TILE), F32), vm((STREAMS, COLORS, QUARTER, TILE), F32),

time: 146 us -> 146 us (level)
  no operation moved by 1% of the time
where the time goes in v16:
time: 146 us
  Pallas kernels  144 us (99%)
  local copies, waits for them, and re-layouts  2.02 us (1%)
    pallas_call x1, Pallas kernels, local_steps(): call(hbm(current), hbm(prec_loc.reshape(1, loc)), hbm(mean_loc.reshape(1,...  144 us

profile of v16, /device:TPU:1, one launch (start us, length us, event | category | flops | bytes accessed | tf_op | source)
XLA Modules:
  0.0 146.2 jit_solution(2649626223648342614)
XLA Ops:
  0.0 144.2 %svgd.1 = f32[2048,512]{1,0:T(8,128)S(1)} custom-call(f32[2048,512]{1,0:T(8,128)} %theta_ref.1, f32[1,512]{1,0:T(1,128)} %bitcast.2, f32[1,512]{1,0:T(1,128)} %bitcast.3, bf16[512,128]{1,0:T(8,128)(2,1)} %fac_hbm.1), custom_call_target="tpu_custom_call" | custom-call | tf_op jit(solution)/shard_map/svgd/pallas_call | solution.py:530
  144.2 2.0 %copy.6 = f32[2048,512]{1,0:T(8,128)} copy(f32[2048,512]{1,0:T(8,128)S(1)} %svgd.1) | data formatting | bytes 8388608

commit v17 on v14

--- a/solution.py
+++ b/solution.py
@@ -329,7 +329,7 @@
                 stot[...] = tot
                 begin([sp_copy()])
             kerns = {}
-            for k in (range(COLORS) if s < 2 else (0, 3, 1, 4, 2, 5)):
+            for k in ((0, 1, 5, 4, 2, 3) if s < 1 else range(COLORS) if s < 2 else (0, 3, 1, 4, 2, 5)):
                 if s < 2:
                     peer, length, keep, give = halves[k][s]
                     rs_copy(st, s, k).wait_recv()

time: 146 us -> 146 us (level)
  no operation moved by 1% of the time
where the time goes in v17:
time: 146 us
  Pallas kernels  144 us (99%)
  local copies, waits for them, and re-layouts  2.02 us (1%)
    pallas_call x1, Pallas kernels, local_steps(): call(hbm(current), hbm(prec_loc.reshape(1, loc)), hbm(mean_loc.reshape(1,...  144 us

profile of v17, /device:TPU:1, one launch (start us, length us, event | category | flops | bytes accessed | tf_op | source)
XLA Modules:
  0.0 145.7 jit_solution(779076186758404479)
XLA Ops:
  0.0 143.7 %svgd.1 = f32[2048,512]{1,0:T(8,128)S(1)} custom-call(f32[2048,512]{1,0:T(8,128)} %theta_ref.1, f32[1,512]{1,0:T(1,128)} %bitcast.2, f32[1,512]{1,0:T(1,128)} %bitcast.3, bf16[512,128]{1,0:T(8,128)(2,1)} %fac_hbm.1), custom_call_target="tpu_custom_call" | custom-call | tf_op jit(solution)/shard_map/svgd/pallas_call | solution.py:527
  143.7 2.0 %copy.6 = f32[2048,512]{1,0:T(8,128)} copy(f32[2048,512]{1,0:T(8,128)S(1)} %svgd.1) | data formatting | bytes 8388608
